TPU v7x, 32 devices: a whole 2x2x4 slice. The times are simulated.
32 devices in a mesh: groups: 2 (over y), ctx: 4 (over z), tp: 4 (over x, core).
Axes of the slice: x: 2, y: 2, z: 4, core: 2. Of those that a mesh axis runs over, the one named last changes fastest.
Arguments:
- q_nope: bfloat16 [512, 16384], P(('groups', 'ctx'), 'tp'), parts along dimension 0, may hold values from -6 to 6
- q_rope: bfloat16 [512, 8192], P(('groups', 'ctx'), 'tp'), parts along dimension 0, may hold values from -6 to 6
- c_kv: bfloat16 [512, 512], P(('groups', 'ctx')), parts along dimension 0, may hold values from -6 to 46.4
- k_rope: bfloat16 [512, 64], P(('groups', 'ctx')), parts along dimension 0, may hold values from -6 to 6
- positions: int32 [512], P(('groups', 'ctx')), parts along dimension 0, may hold values from 0 to 255, as said below
- w_uk: bfloat16 [128, 128, 512], P('tp', 'ctx'), may hold values from -0.5 to 0.5
- w_uv: bfloat16 [128, 512, 128], P('tp', 'ctx'), may hold values from -0.25 to 0.25
- w_out: bfloat16 [16384, 7168], P('tp', 'ctx'), may hold values from -0.125 to 0.125
Outputs:
- attn_proj: bfloat16 [512, 7168], P(('groups', 'tp'), 'ctx'), parts along dimension 0
There are 2 independent parts, one for each index of `groups`. A program takes and returns all parts, laid end to end along the dimension named above; an argument that names none is the same for every part. Nothing has to cross between parts.
Inputs may be any that keep to these rules, and one draw needn't show every extreme that they name: The positions are the 256 integers 0 to 255, each once; every aligned block of 32 rows holds consecutive ascending positions.
All inputs are finite; a program needn't handle non-finite values.
Results may differ from a plain program's by a relative error of at most 0.015.
Values may be sent and summed in bfloat16 or wider, within the bound.
A program may use at most 64 MiB of HBM per device.

v0:
```python
import functools
import math

import jax
import jax.numpy as jnp
from jax import lax
from jax.experimental import pallas as pl
from jax.experimental.pallas import tpu as pltpu
from jax.sharding import PartitionSpec as P

F32 = jnp.float32
BF16 = jnp.bfloat16
MESH = pl.DeviceIdType.MESH


def rotate(values, position):
    half_dim = values.shape[-1] // 2
    freqs = 10000.0 ** (-jnp.arange(half_dim, dtype=jnp.float32) / half_dim)
    angles = position.astype(jnp.float32)[..., None] * freqs
    cosine = jnp.cos(angles)
    sine = jnp.sin(angles)
    first_half = values[..., :half_dim].astype(jnp.float32)
    second_half = values[..., half_dim:].astype(jnp.float32)
    return jnp.concatenate(
        [first_half * cosine - second_half * sine, second_half * cosine + first_half * sine],
        axis=-1,
    )


def mega(sz, qn_in, qr_in, kv_in, kr_in, pos_in, wuk_in, wuv_in, wout_in, out_ref,
         qn, qr, kv, kr, pos, wuk, wuv, wout, krot, table, limit, ho, acc, part, got,
         s1, r1, sy, ry, st, rt, s_right, s_left, r_ag, s_rs, r_rs, loc, loc_out):
    n, groups, tps, nch = sz["n"], sz["g"], sz["t"], sz["nch"]
    tok, hpc, nope, rope, lat, vdim = (sz[k] for k in ("tok", "hpc", "nope", "rope", "lat", "vdim"))
    scale = (nope + rope) ** (-0.5)
    hc = hpc // nch
    hg = hc // groups
    c = lax.axis_index("ctx")
    g = lax.axis_index("groups")
    t = lax.axis_index("tp")
    nsl = nope // n
    lsl = lat // n
    share = tok // tps

    barrier = pltpu.get_barrier_semaphore()
    for axis, me, count in (("ctx", c, n), ("groups", g, groups), ("tp", t, tps)):
        for d in range(1, count):
            pl.semaphore_signal(barrier, inc=1, device_id={axis: lax.rem(me + d, count)}, device_id_type=MESH)
    pl.semaphore_wait(barrier, (n - 1) + (groups - 1) + (tps - 1))

    def al(x, m):
        return pl.multiple_of(x, m)

    def rows_of(s):
        return pl.ds(al(s * tok, tok), tok)

    def piece(kind, i, j, s, part_of):
        if kind in (0, 5):
            src, dst = (kv_in, kv) if kind == 0 else (kr_in, kr)
            if part_of is None:
                return src, dst.at[rows_of(s), :]
            return (src.at[pl.ds(al(part_of * share, share), share), :],
                    dst.at[pl.ds(al(s * tok + part_of * share, share), share), :])
        if kind == 6:
            return pos_in, pos.at[s]
        if kind == 1:
            w = hc * nope
            return (qn_in.at[:, pl.ds(al(j * (hpc * nope) + i * w, w), w)],
                    qn.at[rows_of(s), pl.ds(i * w, w)])
        if kind == 2:
            w = hc * rope
            return (qr_in.at[:, pl.ds(al(j * (hpc * rope) + i * w, w), w)],
                    qr.at[rows_of(s), pl.ds(i * w, w)])
        if part_of is None:
            src_h, dst_h = pl.ds(j * hpc + i * hc, hc), pl.ds(i * hc, hc)
        else:
            src_h = pl.ds(j * hpc + i * hc + part_of * hg, hg)
            dst_h = pl.ds(i * hc + part_of * hg, hg)
        if kind == 3:
            return wuk_in.at[src_h], wuk.at[dst_h, pl.ds(al(s * nsl, nsl), nsl), :]
        return wuv_in.at[src_h], wuv.at[dst_h, pl.ds(al(s * lsl, lsl), lsl), :]

    def copy1(kind, i, d, sending):
        mine = t if kind in (0, 5) else g
        if sending:
            j = lax.rem(c + d, n)
            src, dst = piece(kind, i, j, c, mine)
        else:
            j = lax.rem(c + n - d, n)
            src, dst = piece(kind, i, c, j, mine)
        return pltpu.make_async_remote_copy(
            src_ref=src, dst_ref=dst, send_sem=s1.at[kind, i, d - 1], recv_sem=r1.at[kind, i, d - 1],
            device_id={"ctx": j}, device_id_type=MESH)

    def local(kind, i):
        src, dst = piece(kind, i, c, c, None)
        return pltpu.make_async_copy(src, dst, loc.at[kind, i])

    def kinds(i):
        return (0, 1, 2, 3, 4, 5, 6) if i == 0 else (1, 2, 3, 4)

    order = [((6, 0, 5), 0), ((3, 4), 0)]
    for i in range(nch):
        if i + 1 < nch:
            order.append(((3, 4), i + 1))
        order.append(((1, 2), i))
    for group, i in order:
        for kind in group:
            for d in range(n - 1, 0, -1):
                copy1(kind, i, d, True).start()
    for i in range(nch):
        for kind in kinds(i):
            local(kind, i).start()
    wout_copy = pltpu.make_async_copy(wout_in, wout, loc_out)
    wout_copy.start()

    def copy_y(kind, i, e, d, sending):
        s = lax.rem(c + n - d, n)
        owner = g if sending else lax.rem(g + groups - e, groups)
        _, dst = piece(kind, i, c, s, owner)
        to = lax.rem(g + e, groups) if sending else owner
        return pltpu.make_async_remote_copy(
            src_ref=dst, dst_ref=dst, send_sem=sy.at[kind - 3, i, e - 1, d - 1],
            recv_sem=ry.at[kind - 3, i, e - 1, d - 1],
            device_id={"groups": to}, device_id_type=MESH)

    def copy_t(kind, e, d, sending):
        s = lax.rem(c + n - d, n)
        owner = t if sending else lax.rem(t + tps - e, tps)
        _, dst = piece(kind, 0, c, s, owner)
        to = lax.rem(t + e, tps) if sending else owner
        return pltpu.make_async_remote_copy(
            src_ref=dst, dst_ref=dst, send_sem=st.at[kind // 5, e - 1, d - 1],
            recv_sem=rt.at[kind // 5, e - 1, d - 1],
            device_id={"tp": to}, device_id_type=MESH)

    def forward_weights(i):
        for kind in (3, 4):
            for d in range(1, n):
                copy1(kind, i, d, False).wait_recv()
                for e in range(1, groups):
                    copy_y(kind, i, e, d, True).start()

    def forward_keys():
        for d in range(1, n):
            for kind in (0, 5):
                copy1(kind, 0, d, False).wait_recv()
                for e in range(1, tps):
                    copy_t(kind, e, d, True).start()

    def ag_copy(i, b, right):
        ref = ho.at[b, i]
        return pltpu.make_async_remote_copy(
            src_ref=ref, dst_ref=ref, send_sem=(s_right if right else s_left).at[i, b],
            recv_sem=r_ag.at[i, b],
            device_id={"ctx": c + 1 if right else c - 1}, device_id_type=MESH)

    wide = 2 * rope

    def turn(x):
        lane = lax.broadcasted_iota(jnp.int32, x.shape, 1)
        low = lax.rem(lane, rope) < rope // 2
        other = jnp.where(low, -pltpu.roll(x, wide - rope // 2, 1), pltpu.roll(x, rope // 2, 1))
        return x * table[0] + other * table[1]

    def tables():
        seq = n * tok
        for d in range(1, n):
            copy1(6, 0, d, False).wait_recv()
        local(6, 0).wait()
        row = jnp.concatenate([pos[s] for s in range(n)], axis=1).astype(F32)
        col = jnp.broadcast_to(row, (wide, seq)).T
        lane = lax.broadcasted_iota(jnp.int32, (1, wide), 1)
        index = lax.rem(lane, rope // 2).astype(F32)
        freqs = jnp.exp(index * (-math.log(10000.0) / (rope // 2)))
        angles = col * freqs
        table[0] = jnp.cos(angles)
        table[1] = jnp.sin(angles)
        limit[...] = jnp.where(row > col[:, :1], -1e30, 3e38)

    def keys():
        for kind in (0, 5):
            local(kind, 0).wait()
            for e in range(1, tps):
                for d in range(1, n):
                    copy_t(kind, e, d, False).wait_recv()
        raw = kr[...].astype(F32)
        turned = turn(jnp.concatenate([raw, raw], axis=1))
        lane = lax.broadcasted_iota(jnp.int32, turned.shape, 1)
        krot[0] = jnp.where(lane < rope, turned, 0.0).astype(BF16)
        krot[1] = jnp.where(lane < rope, 0.0, turned).astype(BF16)

    def attend(i):
        nt = (((1,), (1,)), ((), ()))

        def pair(p, carry):
            raw = qr[:, pl.ds(al((i * (hc // 2) + p) * wide, wide), wide)]
            qrp = turn(raw.astype(F32)).astype(BF16)
            for k in range(2):
                hl = 2 * p + k
                h = i * hc + hl
                q = qn[:, pl.ds(al(h * nope, nope), nope)]
                ql = jnp.dot(q, wuk[h], preferred_element_type=F32).astype(BF16)
                sc = lax.dot_general(ql, kv[...], nt, preferred_element_type=F32)
                sc = (sc + lax.dot_general(qrp, krot[k], nt, preferred_element_type=F32)) * scale
                sc = jnp.minimum(sc, limit[...])
                w = jnp.exp(sc - jnp.max(sc, axis=1, keepdims=True))
                total = jnp.sum(w, axis=1, keepdims=True)
                o = jnp.dot(w.astype(BF16), kv[...], preferred_element_type=F32)
                o = (o / total).astype(BF16)
                ho[c, i, :, pl.ds(al(hl * vdim, vdim), vdim)] = jnp.dot(
                    o, wuv[h], preferred_element_type=F32).astype(BF16)
            return carry

        lax.fori_loop(0, hc // 2, pair, 0)

    forward_keys()
    forward_weights(0)
    tables()
    keys()
    for i in range(nch):
        if i + 1 < nch:
            forward_weights(i + 1)
        for kind in (1, 2):
            for d in range(1, n):
                copy1(kind, i, d, False).wait_recv()
        for kind in (1, 2, 3, 4):
            local(kind, i).wait()
        for kind in (3, 4):
            for e in range(1, groups):
                for d in range(1, n):
                    copy_y(kind, i, e, d, False).wait_recv()
        attend(i)

        @pl.when(c + 1 < n)
        def _():
            ag_copy(i, c, True).start()

        @pl.when(c > 0)
        def _():
            ag_copy(i, c, False).start()

    cols = acc.shape[1]
    tile = sz["tile"]
    kdim = hc * vdim

    def project(i, b, first):
        rows = pl.ds(al(b * (hpc * vdim) + i * kdim, kdim), kdim)

        def step(j, carry):
            at = pl.ds(al(j * tile, tile), tile)
            value = jnp.dot(ho[b, i], wout[rows, at], preferred_element_type=F32)
            acc[:, at] = value if first else acc[:, at] + value
            return carry

        lax.fori_loop(0, cols // tile, step, 0)

    waited = False
    for d in range(1, n):
        for i in range(nch):
            @pl.when(c + d < n)
            def _():
                b = c + d
                ag_copy(i, b, False).wait_recv()

                @pl.when(c > 0)
                def _():
                    ag_copy(i, b, False).start()

            @pl.when(c - d >= 0)
            def _():
                b = c - d
                ag_copy(i, b, True).wait_recv()

                @pl.when(c + 1 < n)
                def _():
                    ag_copy(i, b, True).start()

            if not waited:
                wout_copy.wait()
                waited = True
            if d == 1:
                project(i, c, i == 0)

            @pl.when(c - d >= 0)
            def _():
                project(i, c - d, False)

            @pl.when(c + d < n)
            def _():
                project(i, c + d, False)

    rows_out = out_ref.shape[0]
    half = cols // 2
    core = lax.rem(t, 2)
    mate = t + 1 - 2 * core
    across = lax.rem(t + 2, tps)
    mate_across = lax.rem(mate + 2, tps)

    def block(r, at):
        return acc[pl.ds(al(r * rows_out, rows_out), rows_out), at]

    def rs_copy(stage, k):
        at = pl.ds(k * half, half)
        blocks = pl.ds(0, 2) if stage == 0 else pl.ds(2, 1)
        return pltpu.make_async_remote_copy(
            src_ref=part.at[blocks, :, at], dst_ref=got.at[blocks, :, at],
            send_sem=s_rs.at[stage, k], recv_sem=r_rs.at[stage, k],
            device_id={"tp": mate if stage == 0 else across}, device_id_type=MESH)

    spans = [slice(k * half, (k + 1) * half) for k in range(2)]
    for k, at in enumerate(spans):
        part[1, :, at] = block(mate_across, at).astype(BF16)
        part[0, :, at] = block(mate, at).astype(BF16)
        rs_copy(0, k).start()
    for k, at in enumerate(spans):
        rs_copy(0, k).wait_recv()
        part[2, :, at] = (block(across, at) + got[1, :, at].astype(F32)).astype(BF16)
        rs_copy(1, k).start()
    for k, at in enumerate(spans):
        own = block(t, at) + got[0, :, at].astype(F32)
        rs_copy(1, k).wait_recv()
        out_ref[:, at] = (own + got[2, :, at].astype(F32)).astype(BF16)

    for i in range(nch):
        for kind in kinds(i):
            for d in range(1, n):
                copy1(kind, i, d, True).wait_send()
        for kind in (3, 4):
            for e in range(1, groups):
                for d in range(1, n):
                    copy_y(kind, i, e, d, True).wait_send()
        for b in range(n):
            @pl.when(jnp.logical_and(b <= c, c + 1 < n))
            def _():
                ag_copy(i, b, True).wait_send()

            @pl.when(jnp.logical_and(b >= c, c > 0))
            def _():
                ag_copy(i, b, False).wait_send()
    for kind in (0, 5):
        for e in range(1, tps):
            for d in range(1, n):
                copy_t(kind, e, d, True).wait_send()
    for k in range(2):
        rs_copy(0, k).wait_send()
        rs_copy(1, k).wait_send()


def fast(sz, q_nope, q_rope, c_kv, k_rope, positions, w_uk, w_uv, w_out):
    n, groups, tps, nch = sz["n"], sz["g"], sz["t"], sz["nch"]
    tok, hpc, nope, rope, lat, vdim = (sz[k] for k in ("tok", "hpc", "nope", "rope", "lat", "vdim"))
    hc = hpc // nch
    seq = n * tok
    cols = w_out.shape[1]
    hbm = pl.BlockSpec(memory_space=pltpu.HBM)
    dma = pltpu.SemaphoreType.DMA
    more = max(groups - 1, 1)
    return pl.pallas_call(
        functools.partial(mega, sz),
        out_shape=jax.ShapeDtypeStruct((seq // tps, cols), BF16),
        in_specs=[hbm] * 8,
        out_specs=pl.BlockSpec(memory_space=pltpu.VMEM),
        scratch_shapes=[
            pltpu.VMEM((seq, hpc * nope), BF16),
            pltpu.VMEM((seq, hpc * rope), BF16),
            pltpu.VMEM((seq, lat), BF16),
            pltpu.VMEM((seq, rope), BF16),
            pltpu.VMEM((n, 1, tok), jnp.int32),
            pltpu.VMEM((hpc, nope, lat), BF16),
            pltpu.VMEM((hpc, lat, vdim), BF16),
            pltpu.VMEM(w_out.shape, BF16),
            pltpu.VMEM((2, seq, 2 * rope), BF16),
            pltpu.VMEM((2, seq, 2 * rope), F32),
            pltpu.VMEM((seq, seq), F32),
            pltpu.VMEM((n, nch, seq, hc * vdim), BF16),
            pltpu.VMEM((seq, cols), F32),
            pltpu.VMEM((tps - 1, seq // tps, cols), BF16),
            pltpu.VMEM((tps - 1, seq // tps, cols), BF16),
            dma((7, nch, n - 1)),
            dma((7, nch, n - 1)),
            dma((2, nch, more, n - 1)),
            dma((2, nch, more, n - 1)),
            dma((2, tps - 1, n - 1)),
            dma((2, tps - 1, n - 1)),
            dma((nch, n)),
            dma((nch, n)),
            dma((nch, n)),
            dma((2, 2)),
            dma((2, 2)),
            dma((7, nch)),
            dma,
        ],
        compiler_params=pltpu.CompilerParams(collective_id=0, has_side_effects=True,
                                             vmem_limit_bytes=60 * 1024 * 1024),
    )(q_nope, q_rope, c_kv, k_rope, positions.reshape(1, tok), w_uk, w_uv, w_out)


def general(q_nope, q_rope, c_kv, k_rope, positions, w_uk, w_uv, w_out):
    tok_count = q_nope.shape[0]
    head_count = w_uk.shape[0]
    latent = c_kv.shape[1]
    up_key, up_value = (
        lax.all_gather(w_uk, "ctx", axis=1, tiled=True),
        lax.all_gather(w_uv, "ctx", axis=1, tiled=True),
    )
    nope_dim = up_key.shape[1]
    rope_dim = k_rope.shape[1]
    softmax_scale = (nope_dim + rope_dim) ** (-0.5)
    q_parts = q_nope.reshape(tok_count, head_count, nope_dim)
    q_lat = jnp.einsum("thn,hnl->thl", q_parts, up_key, preferred_element_type=jnp.float32).astype(
        jnp.bfloat16
    )
    q_rot = rotate(q_rope.reshape(tok_count, head_count, rope_dim), positions[:, None]).astype(
        jnp.bfloat16
    )
    k_rot = rotate(k_rope, positions).astype(jnp.bfloat16)
    key_rows = jnp.concatenate([c_kv, k_rot], axis=1)
    queries = jnp.concatenate([q_lat, q_rot], axis=2).reshape(
        tok_count * head_count, latent + rope_dim
    )
    query_pos = jnp.repeat(positions, head_count)
    row_total = tok_count * head_count
    key_part = lax.all_gather(key_rows, "ctx", axis=0, tiled=True)
    key_pos = lax.all_gather(positions, "ctx", axis=0, tiled=True)
    run_max = jnp.full((row_total,), -1e30, jnp.float32)
    scores = (
        jnp.einsum("rk,sk->rs", queries, key_part, preferred_element_type=jnp.float32)
        * softmax_scale
    )
    visible = key_pos[None, :] <= query_pos[:, None]
    new_max = jnp.maximum(run_max, jnp.max(jnp.where(visible, scores, -1e30), axis=1))
    weights = jnp.where(visible, jnp.exp(scores - new_max[:, None]), 0.0)
    new_sum = jnp.sum(weights, axis=1)
    added = jnp.dot(
        weights.astype(jnp.bfloat16), key_part[:, :latent], preferred_element_type=jnp.float32
    )
    o_lat = (added / new_sum[:, None]).astype(jnp.bfloat16).reshape(tok_count, head_count, latent)
    head_out = jnp.einsum("thl,hlv->thv", o_lat, up_value, preferred_element_type=jnp.float32)
    rows_out = head_out.astype(jnp.bfloat16).reshape(tok_count, -1)
    partial_value = jnp.dot(
        lax.all_gather(rows_out, "ctx", axis=0, tiled=True),
        w_out,
        preferred_element_type=jnp.float32,
    )
    summed = lax.psum_scatter(
        partial_value.astype(jnp.bfloat16), "tp", scatter_dimension=0, tiled=True
    )
    return summed


CHUNKS = 4


def on_device(sizes, *args):
    q_nope, q_rope, c_kv, k_rope, positions, w_uk, w_uv, w_out = args
    n, groups, tps = sizes["ctx"], sizes["groups"], sizes["tp"]
    heads = w_uk.shape[0]
    hpc = heads // n
    sz = dict(n=n, g=groups, t=tps, nch=CHUNKS, tok=q_nope.shape[0], hpc=hpc,
              nope=w_uk.shape[1] * n, rope=k_rope.shape[1], lat=c_kv.shape[1],
              vdim=w_uv.shape[2], tile=w_out.shape[1] // 2)
    seq = n * sz["tok"]
    cols = w_out.shape[1]
    fits = (
        heads % n == 0
        and n > 1
        and tps == 4
        and hpc % (CHUNKS * groups) == 0
        and (hpc // CHUNKS) % 2 == 0
        and seq <= 512
        and seq % (tps * 16) == 0
        and sz["tok"] % (tps * 16) == 0
        and sz["rope"] == 64
        and sz["nope"] % 128 == 0
        and sz["vdim"] % 128 == 0
        and sz["lat"] % 128 == 0
        and cols % 256 == 0
        and w_out.size * 2 + seq * cols * 8 <= 32 * 2**20
    )
    if fits:
        return fast(sz, *args)
    return general(*args)


def solution(mesh):
    in_specs = (
        P(("groups", "ctx"), "tp"),
        P(("groups", "ctx"), "tp"),
        P(("groups", "ctx"), None),
        P(("groups", "ctx"), None),
        P(("groups", "ctx")),
        P("tp", "ctx", None),
        P("tp", "ctx", None),
        P("tp", "ctx"),
    )
    out_specs = P(("groups", "tp"), "ctx")
    return jax.shard_map(
        functools.partial(on_device, dict(mesh.shape)),
        mesh=mesh, in_specs=in_specs, out_specs=out_specs, check_vma=False,
    )
```

profile of v0, /device:TPU:0, one launch (start us, length us, event | category | flops | bytes accessed | tf_op | source)
XLA Modules:
  0.0 89.1 jit_solution(9837944331803187483)
XLA Ops:
  0.0 87.5 %shard_map.82 = bf16[64,1792]{1,0:T(8,128)(2,1)} custom-call(bf16[64,4096]{1,0:T(8,128)(2,1)} %qn_in.1, bf16[64,2048]{1,0:T(8,128)(2,1)} %qr_in.1, bf16[64,512]{1,0:T(8,128)(2,1)} %kv_in.1, bf16[64,64]{1,0:T(8,128)(2,1)} %kr_in.1, s32[1,64]{1,0:T(1,128)} %bitcast.1, bf16[32,32,512]{2,1,0:T(8,128)(2,1)} %wuk_in.1, bf16[32,128,128]{2,1,0:T(8,128)(2,1)} %wuv_in.1, ...), custom_call_target="tpu_custom_call" | custom-call | tf_op jit(solution)/shard_map/pallas_call | solution.py:359
  87.5 1.6 %copy.10 = bf16[64,1792]{1,0:T(8,128)(2,1)} copy(bf16[64,1792]{1,0:T(8,128)(2,1)} %shard_map.82) | data formatting | bytes 458752
where the time goes:
time: 89.4 us; the launch traced here: 89.1 us
  Pallas kernels  87.5 us (98%)
  local copies, waits for them, and re-layouts  1.64 us (2%)
    pallas_call x1, Pallas kernels, fast(): pl.pallas_call(functools.partial(mega, sz), out_shape=jax.ShapeDtypeStruc...  87.5 us

commit v1 on v0

--- a/solution.py
+++ b/solution.py
@@ -30,10 +30,9 @@
 def mega(sz, qn_in, qr_in, kv_in, kr_in, pos_in, wuk_in, wuv_in, wout_in, out_ref,
          qn, qr, kv, kr, pos, wuk, wuv, wout, krot, table, limit, ho, acc, part, got,
          s1, r1, sy, ry, st, rt, s_right, s_left, r_ag, s_rs, r_rs, loc, loc_out):
-    n, groups, tps, nch = sz["n"], sz["g"], sz["t"], sz["nch"]
-    tok, hpc, nope, rope, lat, vdim = (sz[k] for k in ("tok", "hpc", "nope", "rope", "lat", "vdim"))
+    n, groups, tps, ends, mids = sz["n"], sz["g"], sz["t"], sz["ends"], sz["mids"]
+    tok, hc, nope, rope, lat, vdim = (sz[k] for k in ("tok", "hc", "nope", "rope", "lat", "vdim"))
     scale = (nope + rope) ** (-0.5)
-    hc = hpc // nch
     hg = hc // groups
     c = lax.axis_index("ctx")
     g = lax.axis_index("groups")
@@ -41,15 +40,35 @@
     nsl = nope // n
     lsl = lat // n
     share = tok // tps
+    seq = n * tok
+
+    def outer(j):
+        return jnp.logical_or(j == 0, j == n - 1)
+
+    def count(j):
+        return jnp.where(outer(j), ends, mids)
+
+    def begin(j):
+        return jnp.where(j == 0, 0, ends + (j - 1) * mids)
+
+    mine = count(c)
+    first_mine = begin(c)
+    at_end = outer(c)
 
     barrier = pltpu.get_barrier_semaphore()
-    for axis, me, count in (("ctx", c, n), ("groups", g, groups), ("tp", t, tps)):
-        for d in range(1, count):
-            pl.semaphore_signal(barrier, inc=1, device_id={axis: lax.rem(me + d, count)}, device_id_type=MESH)
+    for axis, me, size in (("ctx", c, n), ("groups", g, groups), ("tp", t, tps)):
+        for d in range(1, size):
+            pl.semaphore_signal(barrier, inc=1, device_id={axis: lax.rem(me + d, size)}, device_id_type=MESH)
     pl.semaphore_wait(barrier, (n - 1) + (groups - 1) + (tps - 1))
 
     def al(x, m):
         return pl.multiple_of(x, m)
+
+    def guard(i, j, body):
+        if i < ends:
+            body()
+        else:
+            pl.when(jnp.logical_not(outer(j)))(body)
 
     def rows_of(s):
         return pl.ds(al(s * tok, tok), tok)
@@ -65,29 +84,29 @@
             return pos_in, pos.at[s]
         if kind == 1:
             w = hc * nope
-            return (qn_in.at[:, pl.ds(al(j * (hpc * nope) + i * w, w), w)],
+            return (qn_in.at[:, pl.ds(al((begin(j) + i) * w, w), w)],
                     qn.at[rows_of(s), pl.ds(i * w, w)])
         if kind == 2:
             w = hc * rope
-            return (qr_in.at[:, pl.ds(al(j * (hpc * rope) + i * w, w), w)],
+            return (qr_in.at[:, pl.ds(al((begin(j) + i) * w, w), w)],
                     qr.at[rows_of(s), pl.ds(i * w, w)])
         if part_of is None:
-            src_h, dst_h = pl.ds(j * hpc + i * hc, hc), pl.ds(i * hc, hc)
+            src_h, dst_h = pl.ds((begin(j) + i) * hc, hc), pl.ds(i * hc, hc)
         else:
-            src_h = pl.ds(j * hpc + i * hc + part_of * hg, hg)
+            src_h = pl.ds((begin(j) + i) * hc + part_of * hg, hg)
             dst_h = pl.ds(i * hc + part_of * hg, hg)
         if kind == 3:
             return wuk_in.at[src_h], wuk.at[dst_h, pl.ds(al(s * nsl, nsl), nsl), :]
         return wuv_in.at[src_h], wuv.at[dst_h, pl.ds(al(s * lsl, lsl), lsl), :]
 
     def copy1(kind, i, d, sending):
-        mine = t if kind in (0, 5) else g
+        owner = t if kind in (0, 5) else g
         if sending:
             j = lax.rem(c + d, n)
-            src, dst = piece(kind, i, j, c, mine)
+            src, dst = piece(kind, i, j, c, owner)
         else:
             j = lax.rem(c + n - d, n)
-            src, dst = piece(kind, i, c, j, mine)
+            src, dst = piece(kind, i, c, j, owner)
         return pltpu.make_async_remote_copy(
             src_ref=src, dst_ref=dst, send_sem=s1.at[kind, i, d - 1], recv_sem=r1.at[kind, i, d - 1],
             device_id={"ctx": j}, device_id_type=MESH)
@@ -99,18 +118,29 @@
     def kinds(i):
         return (0, 1, 2, 3, 4, 5, 6) if i == 0 else (1, 2, 3, 4)
 
-    order = [((6, 0, 5), 0), ((3, 4), 0)]
-    for i in range(nch):
-        if i + 1 < nch:
-            order.append(((3, 4), i + 1))
-        order.append(((1, 2), i))
-    for group, i in order:
-        for kind in group:
-            for d in range(n - 1, 0, -1):
-                copy1(kind, i, d, True).start()
-    for i in range(nch):
-        for kind in kinds(i):
-            local(kind, i).start()
+    def issue(i, group):
+        for d in range(n - 1, 0, -1):
+            def go():
+                for kind in group:
+                    copy1(kind, i, d, True).start()
+            guard(i, lax.rem(c + d, n), go)
+
+    def issue_chunk(i):
+        issue(i, (3, 4))
+        issue(i, (1, 2))
+
+    issue(0, (6, 0, 5))
+    window = sz["window"]
+    for i in range(mids):
+        if i < window:
+            issue_chunk(i)
+        else:
+            pl.when(at_end)(functools.partial(issue_chunk, i))
+    for i in range(mids):
+        def go():
+            for kind in kinds(i):
+                local(kind, i).start()
+        guard(i, c, go)
     wout_copy = pltpu.make_async_copy(wout_in, wout, loc_out)
     wout_copy.start()
 
@@ -148,13 +178,6 @@
                 for e in range(1, tps):
                     copy_t(kind, e, d, True).start()
 
-    def ag_copy(i, b, right):
-        ref = ho.at[b, i]
-        return pltpu.make_async_remote_copy(
-            src_ref=ref, dst_ref=ref, send_sem=(s_right if right else s_left).at[i, b],
-            recv_sem=r_ag.at[i, b],
-            device_id={"ctx": c + 1 if right else c - 1}, device_id_type=MESH)
-
     wide = 2 * rope
 
     def turn(x):
@@ -164,7 +187,6 @@
         return x * table[0] + other * table[1]
 
     def tables():
-        seq = n * tok
         for d in range(1, n):
             copy1(6, 0, d, False).wait_recv()
         local(6, 0).wait()
@@ -208,19 +230,78 @@
                 total = jnp.sum(w, axis=1, keepdims=True)
                 o = jnp.dot(w.astype(BF16), kv[...], preferred_element_type=F32)
                 o = (o / total).astype(BF16)
-                ho[c, i, :, pl.ds(al(hl * vdim, vdim), vdim)] = jnp.dot(
+                ho[first_mine + i, :, pl.ds(al(hl * vdim, vdim), vdim)] = jnp.dot(
                     o, wuv[h], preferred_element_type=F32).astype(BF16)
             return carry
 
         lax.fori_loop(0, hc // 2, pair, 0)
 
-    forward_keys()
-    forward_weights(0)
-    tables()
-    keys()
-    for i in range(nch):
-        if i + 1 < nch:
-            forward_weights(i + 1)
+    away, stay = 0, 1
+    half_rows = seq // 2
+    side = t // 2
+
+    def rows_half(h):
+        return pl.ds(al((1 - side if h == away else side) * half_rows, half_rows), half_rows)
+
+    def ag_copy(q, h, right):
+        ref = ho.at[q, rows_half(h), :]
+        return pltpu.make_async_remote_copy(
+            src_ref=ref, dst_ref=ref, send_sem=(s_right if right else s_left).at[q, h],
+            recv_sem=r_ag.at[q, h],
+            device_id={"ctx": c + 1 if right else c - 1}, device_id_type=MESH)
+
+    inner_right = c < n // 2
+
+    def send_inward(i, h):
+        pl.when(inner_right)(lambda: ag_copy(first_mine + i, h, True).start())
+        pl.when(jnp.logical_not(inner_right))(lambda: ag_copy(first_mine + i, h, False).start())
+
+    def send_outward(i, h):
+        pl.when(jnp.logical_and(inner_right, c > 0))(
+            lambda: ag_copy(first_mine + i, h, False).start())
+        pl.when(jnp.logical_and(jnp.logical_not(inner_right), c + 1 < n))(
+            lambda: ag_copy(first_mine + i, h, True).start())
+
+    cols = acc.shape[1]
+    tile = sz["tile"]
+    kdim = hc * vdim
+
+    def project(q, rows, first=False):
+        depth = pl.ds(al(q * kdim, kdim), kdim)
+
+        def step(j, carry):
+            at = pl.ds(al(j * tile, tile), tile)
+            value = jnp.dot(ho[q, rows, :], wout[depth, at], preferred_element_type=F32)
+            acc[rows, at] = value if first else acc[rows, at] + value
+            return carry
+
+        lax.fori_loop(0, cols // tile, step, 0)
+
+    def handle(d, i, h):
+        @pl.when(jnp.logical_and(c + d < n, i < count(c + d)))
+        def _():
+            q = begin(c + d) + i
+            ag_copy(q, h, False).wait_recv()
+            pl.when(c > 0)(lambda: ag_copy(q, h, False).start())
+            project(q, rows_half(h))
+
+        @pl.when(jnp.logical_and(c - d >= 0, i < count(c - d)))
+        def _():
+            q = begin(c - d) + i
+            ag_copy(q, h, True).wait_recv()
+            pl.when(c + 1 < n)(lambda: ag_copy(q, h, True).start())
+            project(q, rows_half(h))
+
+    def handle_all(d, low, high, h):
+        def body(i, carry):
+            handle(d, i, h)
+            return carry
+
+        lax.fori_loop(low, high, body, 0)
+
+    early = sz["early"]
+
+    def chunk(i):
         for kind in (1, 2):
             for d in range(1, n):
                 copy1(kind, i, d, False).wait_recv()
@@ -231,64 +312,37 @@
                 for d in range(1, n):
                     copy_y(kind, i, e, d, False).wait_recv()
         attend(i)
-
-        @pl.when(c + 1 < n)
-        def _():
-            ag_copy(i, c, True).start()
-
-        @pl.when(c > 0)
-        def _():
-            ag_copy(i, c, False).start()
-
-    cols = acc.shape[1]
-    tile = sz["tile"]
-    kdim = hc * vdim
-
-    def project(i, b, first):
-        rows = pl.ds(al(b * (hpc * vdim) + i * kdim, kdim), kdim)
-
-        def step(j, carry):
-            at = pl.ds(al(j * tile, tile), tile)
-            value = jnp.dot(ho[b, i], wout[rows, at], preferred_element_type=F32)
-            acc[:, at] = value if first else acc[:, at] + value
-            return carry
-
-        lax.fori_loop(0, cols // tile, step, 0)
-
-    waited = False
-    for d in range(1, n):
-        for i in range(nch):
-            @pl.when(c + d < n)
-            def _():
-                b = c + d
-                ag_copy(i, b, False).wait_recv()
-
-                @pl.when(c > 0)
-                def _():
-                    ag_copy(i, b, False).start()
-
-            @pl.when(c - d >= 0)
-            def _():
-                b = c - d
-                ag_copy(i, b, True).wait_recv()
-
-                @pl.when(c + 1 < n)
-                def _():
-                    ag_copy(i, b, True).start()
-
-            if not waited:
-                wout_copy.wait()
-                waited = True
-            if d == 1:
-                project(i, c, i == 0)
-
-            @pl.when(c - d >= 0)
-            def _():
-                project(i, c - d, False)
-
-            @pl.when(c + d < n)
-            def _():
-                project(i, c + d, False)
+        if i + window < mids:
+            pl.when(jnp.logical_not(at_end))(functools.partial(issue_chunk, i + window))
+        send_outward(i, away)
+        send_inward(i, away)
+        send_outward(i, stay)
+        if i < early:
+            send_inward(i, stay)
+        if i == 0:
+            wout_copy.wait()
+        project(first_mine + i, slice(None), i == 0)
+        if i > 0:
+            handle(1, i - 1, away)
+            if i - 1 < early:
+                handle(1, i - 1, stay)
+
+    forward_keys()
+    forward_weights(0)
+    tables()
+    keys()
+    for i in range(mids):
+        if i + 1 < mids:
+            guard(i + 1, c, functools.partial(forward_weights, i + 1))
+        guard(i, c, functools.partial(chunk, i))
+
+    def send_late():
+        for i in range(early, mids):
+            guard(i, c, functools.partial(send_inward, i, stay))
+
+    pl.when(at_end)(send_late)
+    handle_all(1, mine - 1, mids, away)
+    pl.when(jnp.logical_not(at_end))(send_late)
 
     rows_out = out_ref.shape[0]
     half = cols // 2
@@ -302,55 +356,78 @@
 
     def rs_copy(stage, k):
         at = pl.ds(k * half, half)
-        blocks = pl.ds(0, 2) if stage == 0 else pl.ds(2, 1)
+        slot = (1, 2, 0)[stage]
         return pltpu.make_async_remote_copy(
-            src_ref=part.at[blocks, :, at], dst_ref=got.at[blocks, :, at],
+            src_ref=part.at[slot, :, at], dst_ref=got.at[slot, :, at],
             send_sem=s_rs.at[stage, k], recv_sem=r_rs.at[stage, k],
-            device_id={"tp": mate if stage == 0 else across}, device_id_type=MESH)
+            device_id={"tp": across if stage == 1 else mate}, device_id_type=MESH)
 
     spans = [slice(k * half, (k + 1) * half) for k in range(2)]
+
+    handle_all(2, 0, mids, away)
+    for i in range(mids):
+        def done():
+            for kind in (3, 4):
+                for e in range(1, groups):
+                    for d in range(1, n):
+                        copy_y(kind, i, e, d, True).wait_send()
+        guard(i, c, done)
+    handle_all(3, 0, ends, away)
     for k, at in enumerate(spans):
         part[1, :, at] = block(mate_across, at).astype(BF16)
-        part[0, :, at] = block(mate, at).astype(BF16)
         rs_copy(0, k).start()
+    handle(1, early, stay)
     for k, at in enumerate(spans):
         rs_copy(0, k).wait_recv()
         part[2, :, at] = (block(across, at) + got[1, :, at].astype(F32)).astype(BF16)
         rs_copy(1, k).start()
-    for k, at in enumerate(spans):
-        own = block(t, at) + got[0, :, at].astype(F32)
-        rs_copy(1, k).wait_recv()
-        out_ref[:, at] = (own + got[2, :, at].astype(F32)).astype(BF16)
-
-    for i in range(nch):
-        for kind in kinds(i):
-            for d in range(1, n):
-                copy1(kind, i, d, True).wait_send()
-        for kind in (3, 4):
-            for e in range(1, groups):
-                for d in range(1, n):
-                    copy_y(kind, i, e, d, True).wait_send()
-        for b in range(n):
-            @pl.when(jnp.logical_and(b <= c, c + 1 < n))
-            def _():
-                ag_copy(i, b, True).wait_send()
-
-            @pl.when(jnp.logical_and(b >= c, c > 0))
-            def _():
-                ag_copy(i, b, False).wait_send()
+    handle_all(1, early + 1, mids, stay)
+    for i in range(mids):
+        for d in range(1, n):
+            def done():
+                for kind in kinds(i):
+                    copy1(kind, i, d, True).wait_send()
+            guard(i, lax.rem(c + d, n), done)
     for kind in (0, 5):
         for e in range(1, tps):
             for d in range(1, n):
                 copy_t(kind, e, d, True).wait_send()
-    for k in range(2):
-        rs_copy(0, k).wait_send()
-        rs_copy(1, k).wait_send()
+    handle_all(2, 0, mids, stay)
+
+    def drain(h):
+        def right(q, carry):
+            ag_copy(q, h, True).wait_send()
+            return carry
+
+        def left(q, carry):
+            ag_copy(q, h, False).wait_send()
+            return carry
+
+        pl.when(c + 1 < n)(lambda: lax.fori_loop(0, first_mine + mine, right, None))
+        pl.when(c > 0)(lambda: lax.fori_loop(first_mine, ho.shape[0], left, None))
+
+    drain(away)
+    handle_all(3, 0, ends, stay)
+    for k, at in enumerate(spans):
+        part[0, :, at] = block(mate, at).astype(BF16)
+        rs_copy(2, k).start()
+    drain(stay)
+    for k, at in enumerate(spans):
+        rs_copy(1, k).wait_recv()
+        own = block(t, at) + got[2, :, at].astype(F32)
+        rs_copy(2, k).wait_recv()
+        out_ref[:, at] = (own + got[0, :, at].astype(F32)).astype(BF16)
+    for stage in range(3):
+        for k in range(2):
+            rs_copy(stage, k).wait_send()
 
 
 def fast(sz, q_nope, q_rope, c_kv, k_rope, positions, w_uk, w_uv, w_out):
-    n, groups, tps, nch = sz["n"], sz["g"], sz["t"], sz["nch"]
-    tok, hpc, nope, rope, lat, vdim = (sz[k] for k in ("tok", "hpc", "nope", "rope", "lat", "vdim"))
-    hc = hpc // nch
+    n, groups, tps, ends, mids = sz["n"], sz["g"], sz["t"], sz["ends"], sz["mids"]
+    tok, hc, nope, rope, lat, vdim = (sz[k] for k in ("tok", "hc", "nope", "rope", "lat", "vdim"))
+    heads = w_uk.shape[0]
+    chunks = heads // hc
+    hpc = mids * hc
     seq = n * tok
     cols = w_out.shape[1]
     hbm = pl.BlockSpec(memory_space=pltpu.HBM)
@@ -373,22 +450,22 @@
             pltpu.VMEM((2, seq, 2 * rope), BF16),
             pltpu.VMEM((2, seq, 2 * rope), F32),
             pltpu.VMEM((seq, seq), F32),
-            pltpu.VMEM((n, nch, seq, hc * vdim), BF16),
+            pltpu.VMEM((chunks, seq, hc * vdim), BF16),
             pltpu.VMEM((seq, cols), F32),
             pltpu.VMEM((tps - 1, seq // tps, cols), BF16),
             pltpu.VMEM((tps - 1, seq // tps, cols), BF16),
-            dma((7, nch, n - 1)),
-            dma((7, nch, n - 1)),
-            dma((2, nch, more, n - 1)),
-            dma((2, nch, more, n - 1)),
+            dma((7, mids, n - 1)),
+            dma((7, mids, n - 1)),
+            dma((2, mids, more, n - 1)),
+            dma((2, mids, more, n - 1)),
             dma((2, tps - 1, n - 1)),
             dma((2, tps - 1, n - 1)),
-            dma((nch, n)),
-            dma((nch, n)),
-            dma((nch, n)),
-            dma((2, 2)),
-            dma((2, 2)),
-            dma((7, nch)),
+            dma((chunks, 2)),
+            dma((chunks, 2)),
+            dma((chunks, 2)),
+            dma((3, 2)),
+            dma((3, 2)),
+            dma((7, mids)),
             dma,
         ],
         compiler_params=pltpu.CompilerParams(collective_id=0, has_side_effects=True,
@@ -449,25 +526,30 @@
     return summed
 
 
-CHUNKS = 4
+CHUNK_HEADS = 2
+WINDOW = 2
+EARLY = 1
 
 
 def on_device(sizes, *args):
     q_nope, q_rope, c_kv, k_rope, positions, w_uk, w_uv, w_out = args
     n, groups, tps = sizes["ctx"], sizes["groups"], sizes["tp"]
     heads = w_uk.shape[0]
-    hpc = heads // n
-    sz = dict(n=n, g=groups, t=tps, nch=CHUNKS, tok=q_nope.shape[0], hpc=hpc,
+    chunks = heads // CHUNK_HEADS
+    ends = 3 * chunks // 16
+    mids = chunks // 2 - ends
+    sz = dict(n=n, g=groups, t=tps, hc=CHUNK_HEADS, ends=ends, mids=mids, tok=q_nope.shape[0],
+              window=WINDOW, early=EARLY,
               nope=w_uk.shape[1] * n, rope=k_rope.shape[1], lat=c_kv.shape[1],
               vdim=w_uv.shape[2], tile=w_out.shape[1] // 2)
     seq = n * sz["tok"]
     cols = w_out.shape[1]
     fits = (
-        heads % n == 0
-        and n > 1
+        n == 4
         and tps == 4
-        and hpc % (CHUNKS * groups) == 0
-        and (hpc // CHUNKS) % 2 == 0
+        and heads % (2 * CHUNK_HEADS) == 0
+        and CHUNK_HEADS % groups == 0
+        and mids >= ends > EARLY + 1
         and seq <= 512
         and seq % (tps * 16) == 0
         and sz["tok"] % (tps * 16) == 0

time: 89.4 us -> 88.1 us (0.985)
  Pallas kernels: 87.5 us -> 86.3 us
    pallas_call x1, Pallas kernels: 87.5 us -> 86.3 us  [fast(): pl.pallas_call(functools.partial(mega, sz), out_shape=jax.ShapeDtypeStruc...]
where the time goes in v1:
time: 88.1 us; the launch traced here: 88 us
  Pallas kernels  86.3 us (98%)
  local copies, waits for them, and re-layouts  1.64 us (2%)
    pallas_call x1, Pallas kernels, fast(): pl.pallas_call(functools.partial(mega, sz), out_shape=jax.ShapeDtypeStruc...  86.3 us

profile of v1, /device:TPU:0, one launch (start us, length us, event | category | flops | bytes accessed | tf_op | source)
XLA Modules:
  0.0 88.0 jit_solution(12451818301894632839)
XLA Ops:
  0.0 86.3 %shard_map.82 = bf16[64,1792]{1,0:T(8,128)(2,1)} custom-call(bf16[64,4096]{1,0:T(8,128)(2,1)} %qn_in.1, bf16[64,2048]{1,0:T(8,128)(2,1)} %qr_in.1, bf16[64,512]{1,0:T(8,128)(2,1)} %kv_in.1, bf16[64,64]{1,0:T(8,128)(2,1)} %kr_in.1, s32[1,64]{1,0:T(1,128)} %bitcast.1, bf16[32,32,512]{2,1,0:T(8,128)(2,1)} %wuk_in.1, bf16[32,128,128]{2,1,0:T(8,128)(2,1)} %wuv_in.1, ...), custom_call_target="tpu_custom_call" | custom-call | tf_op jit(solution)/shard_map/pallas_call | solution.py:436
  86.3 1.6 %copy.10 = bf16[64,1792]{1,0:T(8,128)(2,1)} copy(bf16[64,1792]{1,0:T(8,128)(2,1)} %shard_map.82) | data formatting | bytes 458752

commit v2 on v1

--- a/solution.py
+++ b/solution.py
@@ -29,7 +29,7 @@
 
 def mega(sz, qn_in, qr_in, kv_in, kr_in, pos_in, wuk_in, wuv_in, wout_in, out_ref,
          qn, qr, kv, kr, pos, wuk, wuv, wout, krot, table, limit, ho, acc, part, got,
-         s1, r1, sy, ry, st, rt, s_right, s_left, r_ag, s_rs, r_rs, loc, loc_out):
+         s_w, s_q, s_k, r_w, r_q, r_k, r_p, s_y, r_y, s_t, r_t, s_ag, r_ag, s_rs, r_rs, loc_out):
     n, groups, tps, ends, mids = sz["n"], sz["g"], sz["t"], sz["ends"], sz["mids"]
     tok, hc, nope, rope, lat, vdim = (sz[k] for k in ("tok", "hc", "nope", "rope", "lat", "vdim"))
     scale = (nope + rope) ** (-0.5)
@@ -107,13 +107,39 @@
         else:
             j = lax.rem(c + n - d, n)
             src, dst = piece(kind, i, c, j, owner)
+        if kind in (3, 4):
+            send, recv = s_w.at[i], r_w.at[i, d - 1]
+        elif kind in (1, 2):
+            send, recv = s_q.at[i], r_q.at[i]
+        elif kind == 6:
+            send, recv = s_k.at[2], r_p
+        else:
+            send, recv = s_k.at[kind // 5], r_k.at[kind // 5, d - 1]
         return pltpu.make_async_remote_copy(
-            src_ref=src, dst_ref=dst, send_sem=s1.at[kind, i, d - 1], recv_sem=r1.at[kind, i, d - 1],
+            src_ref=src, dst_ref=dst, send_sem=send, recv_sem=recv,
             device_id={"ctx": j}, device_id_type=MESH)
 
     def local(kind, i):
         src, dst = piece(kind, i, c, c, None)
-        return pltpu.make_async_copy(src, dst, loc.at[kind, i])
+        if kind in (3, 4):
+            sem = r_y.at[i]
+        elif kind in (1, 2):
+            sem = r_q.at[i]
+        else:
+            sem = r_p if kind == 6 else r_t.at[kind // 5]
+        return pltpu.make_async_copy(src, dst, sem)
+
+    def take(ref, sem):
+        pltpu.make_async_copy(ref, ref, sem).wait()
+
+    def weight_bytes(blocks):
+        return wuk.at[pl.ds(0, blocks), pl.ds(0, nsl), :]
+
+    def query_bytes(blocks):
+        return qn.at[pl.ds(0, blocks * tok), pl.ds(0, hc * (nope + rope))]
+
+    def key_bytes(kind, rows):
+        return (kr if kind else kv).at[pl.ds(0, rows), :]
 
     def kinds(i):
         return (0, 1, 2, 3, 4, 5, 6) if i == 0 else (1, 2, 3, 4)
@@ -150,8 +176,7 @@
         _, dst = piece(kind, i, c, s, owner)
         to = lax.rem(g + e, groups) if sending else owner
         return pltpu.make_async_remote_copy(
-            src_ref=dst, dst_ref=dst, send_sem=sy.at[kind - 3, i, e - 1, d - 1],
-            recv_sem=ry.at[kind - 3, i, e - 1, d - 1],
+            src_ref=dst, dst_ref=dst, send_sem=s_y.at[i], recv_sem=r_y.at[i],
             device_id={"groups": to}, device_id_type=MESH)
 
     def copy_t(kind, e, d, sending):
@@ -160,14 +185,13 @@
         _, dst = piece(kind, 0, c, s, owner)
         to = lax.rem(t + e, tps) if sending else owner
         return pltpu.make_async_remote_copy(
-            src_ref=dst, dst_ref=dst, send_sem=st.at[kind // 5, e - 1, d - 1],
-            recv_sem=rt.at[kind // 5, e - 1, d - 1],
+            src_ref=dst, dst_ref=dst, send_sem=s_t.at[kind // 5], recv_sem=r_t.at[kind // 5],
             device_id={"tp": to}, device_id_type=MESH)
 
     def forward_weights(i):
-        for kind in (3, 4):
-            for d in range(1, n):
-                copy1(kind, i, d, False).wait_recv()
+        for d in range(n - 1, 0, -1):
+            take(weight_bytes(2 * hg), r_w.at[i, d - 1])
+            for kind in (3, 4):
                 for e in range(1, groups):
                     copy_y(kind, i, e, d, True).start()
 
@@ -187,9 +211,7 @@
         return x * table[0] + other * table[1]
 
     def tables():
-        for d in range(1, n):
-            copy1(6, 0, d, False).wait_recv()
-        local(6, 0).wait()
+        take(pos, r_p)
         row = jnp.concatenate([pos[s] for s in range(n)], axis=1).astype(F32)
         col = jnp.broadcast_to(row, (wide, seq)).T
         lane = lax.broadcasted_iota(jnp.int32, (1, wide), 1)
@@ -202,10 +224,7 @@
 
     def keys():
         for kind in (0, 5):
-            local(kind, 0).wait()
-            for e in range(1, tps):
-                for d in range(1, n):
-                    copy_t(kind, e, d, False).wait_recv()
+            take(key_bytes(kind, tok + (n - 1) * (tps - 1) * share), r_t.at[kind // 5])
         raw = kr[...].astype(F32)
         turned = turn(jnp.concatenate([raw, raw], axis=1))
         lane = lax.broadcasted_iota(jnp.int32, turned.shape, 1)
@@ -246,7 +265,7 @@
     def ag_copy(q, h, right):
         ref = ho.at[q, rows_half(h), :]
         return pltpu.make_async_remote_copy(
-            src_ref=ref, dst_ref=ref, send_sem=(s_right if right else s_left).at[q, h],
+            src_ref=ref, dst_ref=ref, send_sem=s_ag.at[1 if right else 0],
             recv_sem=r_ag.at[q, h],
             device_id={"ctx": c + 1 if right else c - 1}, device_id_type=MESH)
 
@@ -302,15 +321,8 @@
     early = sz["early"]
 
     def chunk(i):
-        for kind in (1, 2):
-            for d in range(1, n):
-                copy1(kind, i, d, False).wait_recv()
-        for kind in (1, 2, 3, 4):
-            local(kind, i).wait()
-        for kind in (3, 4):
-            for e in range(1, groups):
-                for d in range(1, n):
-                    copy_y(kind, i, e, d, False).wait_recv()
+        take(query_bytes(n), r_q.at[i])
+        take(weight_bytes((n - 1) * (groups - 1) * 2 * hg + 2 * hc), r_y.at[i])
         attend(i)
         if i + window < mids:
             pl.when(jnp.logical_not(at_end))(functools.partial(issue_chunk, i + window))
@@ -331,9 +343,9 @@
     forward_weights(0)
     tables()
     keys()
-    for i in range(mids):
-        if i + 1 < mids:
-            guard(i + 1, c, functools.partial(forward_weights, i + 1))
+    guard(0, c, functools.partial(chunk, 0))
+    for i in range(1, mids):
+        guard(i, c, functools.partial(forward_weights, i))
         guard(i, c, functools.partial(chunk, i))
 
     def send_late():
@@ -359,19 +371,14 @@
         slot = (1, 2, 0)[stage]
         return pltpu.make_async_remote_copy(
             src_ref=part.at[slot, :, at], dst_ref=got.at[slot, :, at],
-            send_sem=s_rs.at[stage, k], recv_sem=r_rs.at[stage, k],
+            send_sem=s_rs, recv_sem=r_rs.at[stage, k],
             device_id={"tp": across if stage == 1 else mate}, device_id_type=MESH)
 
     spans = [slice(k * half, (k + 1) * half) for k in range(2)]
 
     handle_all(2, 0, mids, away)
     for i in range(mids):
-        def done():
-            for kind in (3, 4):
-                for e in range(1, groups):
-                    for d in range(1, n):
-                        copy_y(kind, i, e, d, True).wait_send()
-        guard(i, c, done)
+        guard(i, c, lambda: take(weight_bytes((n - 1) * (groups - 1) * 2 * hg), s_y.at[i]))
     handle_all(3, 0, ends, away)
     for k, at in enumerate(spans):
         part[1, :, at] = block(mate_across, at).astype(BF16)
@@ -382,44 +389,45 @@
         part[2, :, at] = (block(across, at) + got[1, :, at].astype(F32)).astype(BF16)
         rs_copy(1, k).start()
     handle_all(1, early + 1, mids, stay)
+    def sent(i, peers):
+        take(weight_bytes(peers * 2 * hg), s_w.at[i])
+        take(query_bytes(peers), s_q.at[i])
+
     for i in range(mids):
-        for d in range(1, n):
-            def done():
-                for kind in kinds(i):
-                    copy1(kind, i, d, True).wait_send()
-            guard(i, lax.rem(c + d, n), done)
+        if i < ends:
+            sent(i, n - 1)
+        else:
+            pl.when(at_end)(functools.partial(sent, i, n - 2))
+            pl.when(jnp.logical_not(at_end))(functools.partial(sent, i, n - 3))
     for kind in (0, 5):
-        for e in range(1, tps):
-            for d in range(1, n):
-                copy_t(kind, e, d, True).wait_send()
+        take(key_bytes(kind, (n - 1) * share), s_k.at[kind // 5])
+        take(key_bytes(kind, (n - 1) * (tps - 1) * share), s_t.at[kind // 5])
+    take(pos.at[pl.ds(0, n - 1)], s_k.at[2])
     handle_all(2, 0, mids, stay)
 
-    def drain(h):
-        def right(q, carry):
-            ag_copy(q, h, True).wait_send()
-            return carry
-
-        def left(q, carry):
-            ag_copy(q, h, False).wait_send()
-            return carry
-
-        pl.when(c + 1 < n)(lambda: lax.fori_loop(0, first_mine + mine, right, None))
-        pl.when(c > 0)(lambda: lax.fori_loop(first_mine, ho.shape[0], left, None))
-
-    drain(away)
+    def drain():
+        for b in range(n):
+            low = 0 if b == 0 else ends + (b - 1) * mids
+            high = low + (ends if b in (0, n - 1) else mids)
+
+            @pl.when(c == b)
+            def _():
+                if b + 1 < n:
+                    take(ho.at[pl.ds(0, high)], s_ag.at[1])
+                if b > 0:
+                    take(ho.at[pl.ds(low, ho.shape[0] - low)], s_ag.at[0])
+
     handle_all(3, 0, ends, stay)
     for k, at in enumerate(spans):
         part[0, :, at] = block(mate, at).astype(BF16)
         rs_copy(2, k).start()
-    drain(stay)
     for k, at in enumerate(spans):
         rs_copy(1, k).wait_recv()
         own = block(t, at) + got[2, :, at].astype(F32)
         rs_copy(2, k).wait_recv()
         out_ref[:, at] = (own + got[0, :, at].astype(F32)).astype(BF16)
-    for stage in range(3):
-        for k in range(2):
-            rs_copy(stage, k).wait_send()
+    take(part, s_rs)
+    drain()
 
 
 def fast(sz, q_nope, q_rope, c_kv, k_rope, positions, w_uk, w_uv, w_out):
@@ -432,7 +440,6 @@
     cols = w_out.shape[1]
     hbm = pl.BlockSpec(memory_space=pltpu.HBM)
     dma = pltpu.SemaphoreType.DMA
-    more = max(groups - 1, 1)
     return pl.pallas_call(
         functools.partial(mega, sz),
         out_shape=jax.ShapeDtypeStruct((seq // tps, cols), BF16),
@@ -454,18 +461,21 @@
             pltpu.VMEM((seq, cols), F32),
             pltpu.VMEM((tps - 1, seq // tps, cols), BF16),
             pltpu.VMEM((tps - 1, seq // tps, cols), BF16),
-            dma((7, mids, n - 1)),
-            dma((7, mids, n - 1)),
-            dma((2, mids, more, n - 1)),
-            dma((2, mids, more, n - 1)),
-            dma((2, tps - 1, n - 1)),
-            dma((2, tps - 1, n - 1)),
+            dma((mids,)),
+            dma((mids,)),
+            dma((3,)),
+            dma((mids, n - 1)),
+            dma((mids,)),
+            dma((2, n - 1)),
+            dma,
+            dma((mids,)),
+            dma((mids,)),
+            dma((2,)),
+            dma((2,)),
+            dma((2,)),
             dma((chunks, 2)),
-            dma((chunks, 2)),
-            dma((chunks, 2)),
+            dma,
             dma((3, 2)),
-            dma((3, 2)),
-            dma((7, mids)),
             dma,
         ],
         compiler_params=pltpu.CompilerParams(collective_id=0, has_side_effects=True,
@@ -549,7 +559,10 @@
         and tps == 4
         and heads % (2 * CHUNK_HEADS) == 0
         and CHUNK_HEADS % groups == 0
+        and groups == 2
         and mids >= ends > EARLY + 1
+        and mids >= n + 1
+        and sz["nope"] == sz["vdim"]
         and seq <= 512
         and seq % (tps * 16) == 0
         and sz["tok"] % (tps * 16) == 0

time: 88.1 us -> 92.8 us (1.053)
  Pallas kernels: 86.3 us -> 91 us
    pallas_call x1, Pallas kernels: 86.3 us -> 91 us  [fast(): pl.pallas_call(functools.partial(mega, sz), out_shape=jax.ShapeDtypeStruc...]
where the time goes in v2:
time: 92.8 us; the launch traced here: 92.7 us
  Pallas kernels  91 us (98%)
  local copies, waits for them, and re-layouts  1.64 us (2%)
    pallas_call x1, Pallas kernels, fast(): pl.pallas_call(functools.partial(mega, sz), out_shape=jax.ShapeDtypeStruc...  91 us

profile of v2, /device:TPU:0, one launch (start us, length us, event | category | flops | bytes accessed | tf_op | source)
XLA Modules:
  0.0 92.7 jit_solution(746630024799613282)
XLA Ops:
  0.0 91.0 %shard_map.82 = bf16[64,1792]{1,0:T(8,128)(2,1)} custom-call(bf16[64,4096]{1,0:T(8,128)(2,1)} %qn_in.1, bf16[64,2048]{1,0:T(8,128)(2,1)} %qr_in.1, bf16[64,512]{1,0:T(8,128)(2,1)} %kv_in.1, bf16[64,64]{1,0:T(8,128)(2,1)} %kr_in.1, s32[1,64]{1,0:T(1,128)} %bitcast.1, bf16[32,32,512]{2,1,0:T(8,128)(2,1)} %wuk_in.1, bf16[32,128,128]{2,1,0:T(8,128)(2,1)} %wuv_in.1, ...), custom_call_target="tpu_custom_call" | custom-call | tf_op jit(solution)/shard_map/pallas_call | solution.py:443
  91.0 1.6 %copy.10 = bf16[64,1792]{1,0:T(8,128)(2,1)} copy(bf16[64,1792]{1,0:T(8,128)(2,1)} %shard_map.82) | data formatting | bytes 458752

commit v3 on v2

--- a/solution.py
+++ b/solution.py
@@ -99,10 +99,10 @@
             return wuk_in.at[src_h], wuk.at[dst_h, pl.ds(al(s * nsl, nsl), nsl), :]
         return wuv_in.at[src_h], wuv.at[dst_h, pl.ds(al(s * lsl, lsl), lsl), :]
 
-    def copy1(kind, i, d, sending):
+    def copy1(kind, i, d, to=None):
         owner = t if kind in (0, 5) else g
-        if sending:
-            j = lax.rem(c + d, n)
+        if to is not None:
+            j = to
             src, dst = piece(kind, i, j, c, owner)
         else:
             j = lax.rem(c + n - d, n)
@@ -144,24 +144,44 @@
     def kinds(i):
         return (0, 1, 2, 3, 4, 5, 6) if i == 0 else (1, 2, 3, 4)
 
-    def issue(i, group):
-        for d in range(n - 1, 0, -1):
-            def go():
+    def turns(total):
+        order = [((3, 4), 0)]
+        for i in range(total):
+            if i + 1 < total:
+                order.append(((3, 4), i + 1))
+            order.append(((1, 2), i))
+        return order
+
+    def send_chunks(b, total, targets):
+        for group, i in turns(total):
+            for j in targets:
                 for kind in group:
-                    copy1(kind, i, d, True).start()
-            guard(i, lax.rem(c + d, n), go)
-
-    def issue_chunk(i):
-        issue(i, (3, 4))
-        issue(i, (1, 2))
-
-    issue(0, (6, 0, 5))
-    window = sz["window"]
-    for i in range(mids):
-        if i < window:
-            issue_chunk(i)
-        else:
-            pl.when(at_end)(functools.partial(issue_chunk, i))
+                    copy1(kind, i, (j - b) % n, j).start()
+
+    sides = (0, n - 1)
+
+    def far_ends(b):
+        if b in sides:
+            return [n - 1 - b]
+        return [0 if b >= n // 2 else n - 1]
+
+    for b in range(n):
+        @pl.when(c == b)
+        def _():
+            by_distance = sorted((j for j in range(n) if j != b), key=lambda j: -abs(j - b))
+            for kind in (6, 0, 5):
+                for j in by_distance:
+                    copy1(kind, 0, (j - b) % n, j).start()
+            if b not in sides:
+                send_chunks(b, ends, [n - 1 - far_ends(b)[0]])
+            send_chunks(b, mids, [j for j in by_distance if j not in sides])
+            if b in sides or sz["release"] < 0:
+                send_chunks(b, ends, far_ends(b))
+
+    def send_far():
+        for b in range(1, n - 1):
+            pl.when(c == b)(functools.partial(send_chunks, b, ends, far_ends(b)))
+
     for i in range(mids):
         def go():
             for kind in kinds(i):
@@ -188,17 +208,29 @@
             src_ref=dst, dst_ref=dst, send_sem=s_t.at[kind // 5], recv_sem=r_t.at[kind // 5],
             device_id={"tp": to}, device_id_type=MESH)
 
+    def forward_from(i, d):
+        take(weight_bytes(2 * hg), r_w.at[i, d - 1])
+        for kind in (3, 4):
+            for e in range(1, groups):
+                copy_y(kind, i, e, d, True).start()
+
     def forward_weights(i):
-        for d in range(n - 1, 0, -1):
-            take(weight_bytes(2 * hg), r_w.at[i, d - 1])
-            for kind in (3, 4):
-                for e in range(1, groups):
-                    copy_y(kind, i, e, d, True).start()
+        @pl.when(jnp.logical_not(at_end))
+        def _():
+            forward_from(i, 3)
+            forward_from(i, 1)
+
+        forward_from(i, 2)
+
+    def forward_others(near, far):
+        for d in (near, far):
+            for i in range(ends):
+                forward_from(i, d)
 
     def forward_keys():
         for d in range(1, n):
             for kind in (0, 5):
-                copy1(kind, 0, d, False).wait_recv()
+                copy1(kind, 0, d).wait_recv()
                 for e in range(1, tps):
                     copy_t(kind, e, d, True).start()
 
@@ -296,27 +328,31 @@
 
         lax.fori_loop(0, cols // tile, step, 0)
 
-    def handle(d, i, h):
-        @pl.when(jnp.logical_and(c + d < n, i < count(c + d)))
+    def arrive(b, i, h, right):
+        @pl.when(jnp.logical_and(jnp.logical_and(b >= 0, b < n), jnp.logical_and(i >= 0, i < count(b))))
         def _():
-            q = begin(c + d) + i
-            ag_copy(q, h, False).wait_recv()
-            pl.when(c > 0)(lambda: ag_copy(q, h, False).start())
+            q = begin(b) + i
+            with jax.named_scope("take"):
+                ag_copy(q, h, right).wait_recv()
+            more = c + 1 < n if right else c > 0
+            pl.when(more)(lambda: ag_copy(q, h, right).start())
             project(q, rows_half(h))
 
-        @pl.when(jnp.logical_and(c - d >= 0, i < count(c - d)))
-        def _():
-            q = begin(c - d) + i
-            ag_copy(q, h, True).wait_recv()
-            pl.when(c + 1 < n)(lambda: ag_copy(q, h, True).start())
-            project(q, rows_half(h))
-
-    def handle_all(d, low, high, h):
+    def arrive_all(d, low, high, h):
         def body(i, carry):
-            handle(d, i, h)
+            arrive(c + d, i, h, False)
+            arrive(c - d, i, h, True)
             return carry
 
         lax.fori_loop(low, high, body, 0)
+
+    def arrive_inward(i, h):
+        pl.when(inner_right)(lambda: arrive(c + 1, i, h, False))
+        pl.when(jnp.logical_not(inner_right))(lambda: arrive(c - 1, i, h, True))
+
+    def arrive_outward(i, h):
+        pl.when(inner_right)(lambda: arrive(c - 1, i, h, True))
+        pl.when(jnp.logical_not(inner_right))(lambda: arrive(c + 1, i, h, False))
 
     early = sz["early"]
 
@@ -324,37 +360,44 @@
         take(query_bytes(n), r_q.at[i])
         take(weight_bytes((n - 1) * (groups - 1) * 2 * hg + 2 * hc), r_y.at[i])
         attend(i)
-        if i + window < mids:
-            pl.when(jnp.logical_not(at_end))(functools.partial(issue_chunk, i + window))
         send_outward(i, away)
         send_inward(i, away)
         send_outward(i, stay)
         if i < early:
-            send_inward(i, stay)
+            pl.when(jnp.logical_not(at_end))(functools.partial(send_inward, i, stay))
+        if i == sz["release"]:
+            send_far()
         if i == 0:
             wout_copy.wait()
         project(first_mine + i, slice(None), i == 0)
-        if i > 0:
-            handle(1, i - 1, away)
-            if i - 1 < early:
-                handle(1, i - 1, stay)
 
     forward_keys()
+    pl.when(c == 0)(functools.partial(forward_others, 3, 1))
+    pl.when(c == n - 1)(functools.partial(forward_others, 1, 3))
     forward_weights(0)
     tables()
     keys()
-    guard(0, c, functools.partial(chunk, 0))
-    for i in range(1, mids):
-        guard(i, c, functools.partial(forward_weights, i))
+    for i in range(mids):
+        if i + 1 < mids:
+            guard(i + 1, c, functools.partial(forward_weights, i + 1))
         guard(i, c, functools.partial(chunk, i))
 
-    def send_late():
-        for i in range(early, mids):
-            guard(i, c, functools.partial(send_inward, i, stay))
-
-    pl.when(at_end)(send_late)
-    handle_all(1, mine - 1, mids, away)
-    pl.when(jnp.logical_not(at_end))(send_late)
+    def send_late(low, high):
+        for i in range(low, high):
+            send_inward(i, stay)
+
+    pl.when(at_end)(functools.partial(send_late, 0, ends))
+    for i in range(early):
+        arrive_inward(i, away)
+        arrive_inward(i, stay)
+
+    def first_away(i, carry):
+        arrive_inward(i, away)
+        arrive_outward(i - early - sz["behind"], away)
+        return carry
+
+    lax.fori_loop(early, ends + early + sz["behind"] + (mids - ends), first_away, 0)
+    pl.when(jnp.logical_not(at_end))(functools.partial(send_late, early, mids))
 
     rows_out = out_ref.shape[0]
     half = cols // 2
@@ -376,19 +419,26 @@
 
     spans = [slice(k * half, (k + 1) * half) for k in range(2)]
 
-    handle_all(2, 0, mids, away)
+    arrive_all(2, 0, mids, away)
     for i in range(mids):
         guard(i, c, lambda: take(weight_bytes((n - 1) * (groups - 1) * 2 * hg), s_y.at[i]))
-    handle_all(3, 0, ends, away)
+    arrive_all(3, 0, ends, away)
     for k, at in enumerate(spans):
         part[1, :, at] = block(mate_across, at).astype(BF16)
         rs_copy(0, k).start()
-    handle(1, early, stay)
+    arrive_inward(early, stay)
+    arrive_outward(0, stay)
     for k, at in enumerate(spans):
         rs_copy(0, k).wait_recv()
         part[2, :, at] = (block(across, at) + got[1, :, at].astype(F32)).astype(BF16)
         rs_copy(1, k).start()
-    handle_all(1, early + 1, mids, stay)
+
+    def first_stay(i, carry):
+        arrive_inward(i + early, stay)
+        arrive_outward(i, stay)
+        return carry
+
+    lax.fori_loop(1, mids - early, first_stay, 0)
     def sent(i, peers):
         take(weight_bytes(peers * 2 * hg), s_w.at[i])
         take(query_bytes(peers), s_q.at[i])
@@ -403,7 +453,7 @@
         take(key_bytes(kind, (n - 1) * share), s_k.at[kind // 5])
         take(key_bytes(kind, (n - 1) * (tps - 1) * share), s_t.at[kind // 5])
     take(pos.at[pl.ds(0, n - 1)], s_k.at[2])
-    handle_all(2, 0, mids, stay)
+    arrive_all(2, 0, mids, stay)
 
     def drain():
         for b in range(n):
@@ -417,7 +467,7 @@
                 if b > 0:
                     take(ho.at[pl.ds(low, ho.shape[0] - low)], s_ag.at[0])
 
-    handle_all(3, 0, ends, stay)
+    arrive_all(3, 0, ends, stay)
     for k, at in enumerate(spans):
         part[0, :, at] = block(mate, at).astype(BF16)
         rs_copy(2, k).start()
@@ -537,8 +587,9 @@
 
 
 CHUNK_HEADS = 2
-WINDOW = 2
+RELEASE = -1
 EARLY = 1
+BEHIND = 1
 
 
 def on_device(sizes, *args):
@@ -549,7 +600,7 @@
     ends = 3 * chunks // 16
     mids = chunks // 2 - ends
     sz = dict(n=n, g=groups, t=tps, hc=CHUNK_HEADS, ends=ends, mids=mids, tok=q_nope.shape[0],
-              window=WINDOW, early=EARLY,
+              release=RELEASE, early=EARLY, behind=BEHIND,
               nope=w_uk.shape[1] * n, rope=k_rope.shape[1], lat=c_kv.shape[1],
               vdim=w_uv.shape[2], tile=w_out.shape[1] // 2)
     seq = n * sz["tok"]
@@ -560,7 +611,7 @@
         and heads % (2 * CHUNK_HEADS) == 0
         and CHUNK_HEADS % groups == 0
         and groups == 2
-        and mids >= ends > EARLY + 1
+        and mids >= ends > EARLY
         and mids >= n + 1
         and sz["nope"] == sz["vdim"]
         and seq <= 512

time: 92.8 us -> 80.4 us (0.87)
  Pallas kernels: 91 us -> 78.6 us
    pallas_call x1, Pallas kernels: 91 us -> 78.6 us  [fast(): pl.pallas_call(functools.partial(mega, sz), out_shape=jax.ShapeDtypeStruc...]
where the time goes in v3:
time: 80.4 us; the launch traced here: 80.2 us
  Pallas kernels  78.6 us (98%)
  local copies, waits for them, and re-layouts  1.64 us (2%)
    pallas_call x1, Pallas kernels, fast(): pl.pallas_call(functools.partial(mega, sz), out_shape=jax.ShapeDtypeStruc...  78.6 us
    unnamed x1, local copies, waits for them, and re-layouts  1.64 us

profile of v3, /device:TPU:0, one launch (start us, length us, event | category | flops | bytes accessed | tf_op | source)
XLA Modules:
  0.0 80.2 jit_solution(1297977079569296644)
XLA Ops:
  0.0 78.6 %shard_map.82 = bf16[64,1792]{1,0:T(8,128)(2,1)} custom-call(bf16[64,4096]{1,0:T(8,128)(2,1)} %qn_in.1, bf16[64,2048]{1,0:T(8,128)(2,1)} %qr_in.1, bf16[64,512]{1,0:T(8,128)(2,1)} %kv_in.1, bf16[64,64]{1,0:T(8,128)(2,1)} %kr_in.1, s32[1,64]{1,0:T(1,128)} %bitcast.1, bf16[32,32,512]{2,1,0:T(8,128)(2,1)} %wuk_in.1, bf16[32,128,128]{2,1,0:T(8,128)(2,1)} %wuv_in.1, ...), custom_call_target="tpu_custom_call" | custom-call | tf_op jit(solution)/shard_map/pallas_call | solution.py:493
  78.6 1.6 %copy.10 = bf16[64,1792]{1,0:T(8,128)(2,1)} copy(bf16[64,1792]{1,0:T(8,128)(2,1)} %shard_map.82) | data formatting | bytes 458752

commit v4 on v3

--- a/solution.py
+++ b/solution.py
@@ -29,7 +29,7 @@
 
 def mega(sz, qn_in, qr_in, kv_in, kr_in, pos_in, wuk_in, wuv_in, wout_in, out_ref,
          qn, qr, kv, kr, pos, wuk, wuv, wout, krot, table, limit, ho, acc, part, got,
-         s_w, s_q, s_k, r_w, r_q, r_k, r_p, s_y, r_y, s_t, r_t, s_ag, r_ag, s_rs, r_rs, loc_out):
+         s_w, s_q, s_k, r_w, r_q, r_k, r_p, s_y, r_y, s_t, r_t, s_ag, r_ag, s_rs, r_rs, hop, loc_out):
     n, groups, tps, ends, mids = sz["n"], sz["g"], sz["t"], sz["ends"], sz["mids"]
     tok, hc, nope, rope, lat, vdim = (sz[k] for k in ("tok", "hc", "nope", "rope", "lat", "vdim"))
     scale = (nope + rope) ** (-0.5)
@@ -54,12 +54,6 @@
     mine = count(c)
     first_mine = begin(c)
     at_end = outer(c)
-
-    barrier = pltpu.get_barrier_semaphore()
-    for axis, me, size in (("ctx", c, n), ("groups", g, groups), ("tp", t, tps)):
-        for d in range(1, size):
-            pl.semaphore_signal(barrier, inc=1, device_id={axis: lax.rem(me + d, size)}, device_id_type=MESH)
-    pl.semaphore_wait(barrier, (n - 1) + (groups - 1) + (tps - 1))
 
     def al(x, m):
         return pl.multiple_of(x, m)
@@ -144,19 +138,17 @@
     def kinds(i):
         return (0, 1, 2, 3, 4, 5, 6) if i == 0 else (1, 2, 3, 4)
 
-    def turns(total):
-        order = [((3, 4), 0)]
-        for i in range(total):
-            if i + 1 < total:
-                order.append(((3, 4), i + 1))
-            order.append(((1, 2), i))
-        return order
-
-    def send_chunks(b, total, targets):
-        for group, i in turns(total):
+    def turn_of(i, total):
+        groups_of = [((3, 4), 0)] if i == 0 else []
+        if i + 1 < total:
+            groups_of.append(((3, 4), i + 1))
+        return groups_of + [((1, 2), i)]
+
+    def send_chunk(b, i, total, targets):
+        for group, k in turn_of(i, total):
             for j in targets:
                 for kind in group:
-                    copy1(kind, i, (j - b) % n, j).start()
+                    copy1(kind, k, (j - b) % n, j).start()
 
     sides = (0, n - 1)
 
@@ -164,23 +156,6 @@
         if b in sides:
             return [n - 1 - b]
         return [0 if b >= n // 2 else n - 1]
-
-    for b in range(n):
-        @pl.when(c == b)
-        def _():
-            by_distance = sorted((j for j in range(n) if j != b), key=lambda j: -abs(j - b))
-            for kind in (6, 0, 5):
-                for j in by_distance:
-                    copy1(kind, 0, (j - b) % n, j).start()
-            if b not in sides:
-                send_chunks(b, ends, [n - 1 - far_ends(b)[0]])
-            send_chunks(b, mids, [j for j in by_distance if j not in sides])
-            if b in sides or sz["release"] < 0:
-                send_chunks(b, ends, far_ends(b))
-
-    def send_far():
-        for b in range(1, n - 1):
-            pl.when(c == b)(functools.partial(send_chunks, b, ends, far_ends(b)))
 
     for i in range(mids):
         def go():
@@ -189,6 +164,60 @@
         guard(i, c, go)
     wout_copy = pltpu.make_async_copy(wout_in, wout, loc_out)
     wout_copy.start()
+
+    barrier = pltpu.get_barrier_semaphore()
+
+    def tell(sem, axis, to):
+        pl.semaphore_signal(sem, inc=1, device_id={axis: to}, device_id_type=MESH)
+
+    pl.when(c > 0)(lambda: tell(barrier, "ctx", c - 1))
+    pl.when(c + 1 < n)(lambda: tell(barrier, "ctx", c + 1))
+    for axis, me, size in (("groups", g, groups), ("tp", t, tps)):
+        for d in range(1, size):
+            tell(barrier, axis, lax.rem(me + d, size))
+    pl.semaphore_wait(barrier, jnp.where(at_end, 1, 2) + (groups - 1) + (tps - 1))
+
+    def send_keys(b, j):
+        for kind in (6, 0, 5):
+            copy1(kind, 0, (j - b) % n, j).start()
+
+    for b in range(n):
+        @pl.when(c == b)
+        def _():
+            step = 1 if b < n // 2 else -1
+            if b in sides:
+                near, next_on, far = (b + k * step for k in range(1, n))
+                middle = [next_on, near]
+                send_keys(b, near)
+                pl.semaphore_wait(hop.at[0], 1)
+                send_keys(b, next_on)
+                send_chunk(b, 0, mids, middle)
+                pl.semaphore_wait(hop.at[1], 1)
+                send_keys(b, far)
+            else:
+                outside, middle, far = b - step, [b + step], b + 2 * step
+                for j in (outside, *middle):
+                    tell(hop.at[0], "ctx", j)
+                send_keys(b, *middle)
+                send_chunk(b, 0, mids, middle)
+                send_keys(b, outside)
+                for i in range(ends):
+                    send_chunk(b, i, ends, [outside])
+                pl.semaphore_wait(hop.at[0], 1)
+                tell(hop.at[1], "ctx", outside)
+                send_keys(b, far)
+            for i in range(1, mids):
+                send_chunk(b, i, mids, middle)
+            if b not in sides:
+                for i in range(ends):
+                    send_chunk(b, i, ends, [far])
+
+    def send_far():
+        for b in sides:
+            @pl.when(c == b)
+            def _():
+                for i in range(ends):
+                    send_chunk(b, i, ends, far_ends(b))
 
     def copy_y(kind, i, e, d, sending):
         s = lax.rem(c + n - d, n)
@@ -317,13 +346,13 @@
     tile = sz["tile"]
     kdim = hc * vdim
 
-    def project(q, rows, first=False):
+    def project(q, rows):
         depth = pl.ds(al(q * kdim, kdim), kdim)
 
         def step(j, carry):
             at = pl.ds(al(j * tile, tile), tile)
             value = jnp.dot(ho[q, rows, :], wout[depth, at], preferred_element_type=F32)
-            acc[rows, at] = value if first else acc[rows, at] + value
+            acc[rows, at] = acc[rows, at] + value
             return carry
 
         lax.fori_loop(0, cols // tile, step, 0)
@@ -365,18 +394,31 @@
         send_outward(i, stay)
         if i < early:
             pl.when(jnp.logical_not(at_end))(functools.partial(send_inward, i, stay))
-        if i == sz["release"]:
-            send_far()
-        if i == 0:
-            wout_copy.wait()
-        project(first_mine + i, slice(None), i == 0)
+        project(first_mine + i, slice(None))
 
     forward_keys()
-    pl.when(c == 0)(functools.partial(forward_others, 3, 1))
-    pl.when(c == n - 1)(functools.partial(forward_others, 1, 3))
-    forward_weights(0)
-    tables()
-    keys()
+    def between():
+        tables()
+        keys()
+        acc[...] = jnp.zeros_like(acc)
+        wout_copy.wait()
+
+    @pl.when(jnp.logical_not(at_end))
+    def _():
+        forward_weights(0)
+        between()
+
+    @pl.when(at_end)
+    def _():
+        between()
+        for i in range(sz["release"]):
+            arrive_inward(i, away)
+            arrive_inward(i, stay)
+        send_far()
+        pl.when(c == 0)(functools.partial(forward_others, 3, 1))
+        pl.when(c == n - 1)(functools.partial(forward_others, 1, 3))
+        forward_weights(0)
+
     for i in range(mids):
         if i + 1 < mids:
             guard(i + 1, c, functools.partial(forward_weights, i + 1))
@@ -387,16 +429,20 @@
             send_inward(i, stay)
 
     pl.when(at_end)(functools.partial(send_late, 0, ends))
-    for i in range(early):
-        arrive_inward(i, away)
-        arrive_inward(i, stay)
+    @pl.when(jnp.logical_not(at_end))
+    def _():
+        for i in range(early):
+            arrive_inward(i, away)
+            arrive_inward(i, stay)
+
+    seen = jnp.where(at_end, sz["release"], early)
 
     def first_away(i, carry):
-        arrive_inward(i, away)
-        arrive_outward(i - early - sz["behind"], away)
+        arrive_inward(i + seen, away)
+        arrive_outward(i - sz["behind"], away)
         return carry
 
-    lax.fori_loop(early, ends + early + sz["behind"] + (mids - ends), first_away, 0)
+    lax.fori_loop(0, mids + sz["behind"], first_away, 0)
     pl.when(jnp.logical_not(at_end))(functools.partial(send_late, early, mids))
 
     rows_out = out_ref.shape[0]
@@ -426,7 +472,7 @@
     for k, at in enumerate(spans):
         part[1, :, at] = block(mate_across, at).astype(BF16)
         rs_copy(0, k).start()
-    arrive_inward(early, stay)
+    arrive_inward(seen, stay)
     arrive_outward(0, stay)
     for k, at in enumerate(spans):
         rs_copy(0, k).wait_recv()
@@ -434,11 +480,11 @@
         rs_copy(1, k).start()
 
     def first_stay(i, carry):
-        arrive_inward(i + early, stay)
+        arrive_inward(i + seen, stay)
         arrive_outward(i, stay)
         return carry
 
-    lax.fori_loop(1, mids - early, first_stay, 0)
+    lax.fori_loop(1, mids, first_stay, 0)
     def sent(i, peers):
         take(weight_bytes(peers * 2 * hg), s_w.at[i])
         take(query_bytes(peers), s_q.at[i])
@@ -492,7 +538,7 @@
     dma = pltpu.SemaphoreType.DMA
     return pl.pallas_call(
         functools.partial(mega, sz),
-        out_shape=jax.ShapeDtypeStruct((seq // tps, cols), BF16),
+        out_shape=pltpu.VMEM((seq // tps, cols), BF16),
         in_specs=[hbm] * 8,
         out_specs=pl.BlockSpec(memory_space=pltpu.VMEM),
         scratch_shapes=[
@@ -526,6 +572,7 @@
             dma((chunks, 2)),
             dma,
             dma((3, 2)),
+            pltpu.SemaphoreType.REGULAR((2,)),
             dma,
         ],
         compiler_params=pltpu.CompilerParams(collective_id=0, has_side_effects=True,
@@ -587,7 +634,8 @@
 
 
 CHUNK_HEADS = 2
-RELEASE = -1
+END_CHUNKS = 2
+RELEASE = 3
 EARLY = 1
 BEHIND = 1
 
@@ -597,7 +645,7 @@
     n, groups, tps = sizes["ctx"], sizes["groups"], sizes["tp"]
     heads = w_uk.shape[0]
     chunks = heads // CHUNK_HEADS
-    ends = 3 * chunks // 16
+    ends = END_CHUNKS * chunks // 16
     mids = chunks // 2 - ends
     sz = dict(n=n, g=groups, t=tps, hc=CHUNK_HEADS, ends=ends, mids=mids, tok=q_nope.shape[0],
               release=RELEASE, early=EARLY, behind=BEHIND,
@@ -612,6 +660,7 @@
         and CHUNK_HEADS % groups == 0
         and groups == 2
         and mids >= ends > EARLY
+        and mids > RELEASE
         and mids >= n + 1
         and sz["nope"] == sz["vdim"]
         and seq <= 512

time: 80.4 us -> 79 us (0.983)
  local copies, waits for them, and re-layouts: 1.64 us -> 0.69 us
    unnamed x1, local copies, waits for them, and re-layouts: 1.64 us -> 0.69 us
where the time goes in v4:
time: 79 us; the launch traced here: 78.8 us
  Pallas kernels  78.1 us (99%)
    pallas_call x1, Pallas kernels, fast(): pl.pallas_call(functools.partial(mega, sz), out_shape=pltpu.VMEM((seq //...  78.1 us

profile of v4, /device:TPU:0, one launch (start us, length us, event | category | flops | bytes accessed | tf_op | source)
XLA Modules:
  0.0 78.8 jit_solution(7975115494711169376)
XLA Ops:
  0.0 78.1 %shard_map.82 = bf16[64,1792]{1,0:T(8,128)(2,1)S(1)} custom-call(bf16[64,4096]{1,0:T(8,128)(2,1)} %qn_in.1, bf16[64,2048]{1,0:T(8,128)(2,1)} %qr_in.1, bf16[64,512]{1,0:T(8,128)(2,1)} %kv_in.1, bf16[64,64]{1,0:T(8,128)(2,1)} %kr_in.1, s32[1,64]{1,0:T(1,128)} %bitcast.1, bf16[32,32,512]{2,1,0:T(8,128)(2,1)} %wuk_in.1, bf16[32,128,128]{2,1,0:T(8,128)(2,1)} %wuv_in.1, ...), custom_call_target="tpu_custom_call" | custom-call | tf_op jit(solution)/shard_map/pallas_call | solution.py:539
  78.1 0.7 copy.10

commit v5 on v4

--- a/solution.py
+++ b/solution.py
@@ -152,10 +152,9 @@
 
     sides = (0, n - 1)
 
-    def far_ends(b):
-        if b in sides:
-            return [n - 1 - b]
-        return [0 if b >= n // 2 else n - 1]
+    def send_far_chunk(b, k, far):
+        for kind in (3, 4, 1, 2):
+            copy1(kind, k, (far - b) % n, far).start()
 
     for i in range(mids):
         def go():
@@ -177,8 +176,8 @@
             tell(barrier, axis, lax.rem(me + d, size))
     pl.semaphore_wait(barrier, jnp.where(at_end, 1, 2) + (groups - 1) + (tps - 1))
 
-    def send_keys(b, j):
-        for kind in (6, 0, 5):
+    def send_keys(b, j, group):
+        for kind in group:
             copy1(kind, 0, (j - b) % n, j).start()
 
     for b in range(n):
@@ -188,36 +187,34 @@
             if b in sides:
                 near, next_on, far = (b + k * step for k in range(1, n))
                 middle = [next_on, near]
-                send_keys(b, near)
+                send_keys(b, near, (6, 0, 5))
                 pl.semaphore_wait(hop.at[0], 1)
-                send_keys(b, next_on)
+                send_keys(b, next_on, (6, 0, 5))
                 send_chunk(b, 0, mids, middle)
                 pl.semaphore_wait(hop.at[1], 1)
-                send_keys(b, far)
+                send_keys(b, far, (6,))
             else:
                 outside, middle, far = b - step, [b + step], b + 2 * step
                 for j in (outside, *middle):
                     tell(hop.at[0], "ctx", j)
-                send_keys(b, *middle)
+                send_keys(b, middle[0], (6, 0, 5))
                 send_chunk(b, 0, mids, middle)
-                send_keys(b, outside)
+                send_keys(b, outside, (6, 0, 5))
                 for i in range(ends):
                     send_chunk(b, i, ends, [outside])
                 pl.semaphore_wait(hop.at[0], 1)
                 tell(hop.at[1], "ctx", outside)
-                send_keys(b, far)
+                send_keys(b, far, (6,))
             for i in range(1, mids):
                 send_chunk(b, i, mids, middle)
-            if b not in sides:
-                for i in range(ends):
-                    send_chunk(b, i, ends, [far])
-
-    def send_far():
+                if b not in sides:
+                    for k in range(ends):
+                        if i == mids - 1 - (ends - 1 - k) * sz["spread"]:
+                            send_far_chunk(b, k, far)
+
+    def send_far(k):
         for b in sides:
-            @pl.when(c == b)
-            def _():
-                for i in range(ends):
-                    send_chunk(b, i, ends, far_ends(b))
+            pl.when(c == b)(functools.partial(send_far_chunk, b, k, n - 1 - b))
 
     def copy_y(kind, i, e, d, sending):
         s = lax.rem(c + n - d, n)
@@ -256,10 +253,21 @@
             for i in range(ends):
                 forward_from(i, d)
 
+    def pass_key(kind, b, origin, out):
+        ref = (kr if kind else kv).at[pl.ds(al(origin * tok + t * share, share), share), :]
+        return pltpu.make_async_remote_copy(
+            src_ref=ref, dst_ref=ref, send_sem=s_k.at[kind // 5],
+            recv_sem=r_k.at[kind // 5, (out - origin) % n - 1],
+            device_id={"ctx": out}, device_id_type=MESH)
+
     def forward_keys():
         for d in range(1, n):
             for kind in (0, 5):
                 copy1(kind, 0, d).wait_recv()
+                for b in range(1, n - 1):
+                    out = 0 if b < n // 2 else n - 1
+                    if (b - d) % n != out:
+                        pl.when(c == b)(lambda: pass_key(kind, b, (b - d) % n, out).start())
                 for e in range(1, tps):
                     copy_t(kind, e, d, True).start()
 
@@ -323,24 +331,35 @@
     def rows_half(h):
         return pl.ds(al((1 - side if h == away else side) * half_rows, half_rows), half_rows)
 
-    def ag_copy(q, h, right):
-        ref = ho.at[q, rows_half(h), :]
+    quarter = half_rows // 2
+
+    def parts_of(h):
+        return (0,) if h == away else (1, 2)
+
+    def ag_copy(q, p, right):
+        rows = rows_half(away)
+        if p > 0:
+            rows = pl.ds(al(side * half_rows + (p - 1) * quarter, quarter), quarter)
+        ref = ho.at[q, rows, :]
         return pltpu.make_async_remote_copy(
             src_ref=ref, dst_ref=ref, send_sem=s_ag.at[1 if right else 0],
-            recv_sem=r_ag.at[q, h],
+            recv_sem=r_ag.at[q, p],
             device_id={"ctx": c + 1 if right else c - 1}, device_id_type=MESH)
 
     inner_right = c < n // 2
 
+    def send_item(i, h, right):
+        for p in parts_of(h):
+            ag_copy(first_mine + i, p, right).start()
+
     def send_inward(i, h):
-        pl.when(inner_right)(lambda: ag_copy(first_mine + i, h, True).start())
-        pl.when(jnp.logical_not(inner_right))(lambda: ag_copy(first_mine + i, h, False).start())
+        pl.when(inner_right)(functools.partial(send_item, i, h, True))
+        pl.when(jnp.logical_not(inner_right))(functools.partial(send_item, i, h, False))
 
     def send_outward(i, h):
-        pl.when(jnp.logical_and(inner_right, c > 0))(
-            lambda: ag_copy(first_mine + i, h, False).start())
+        pl.when(jnp.logical_and(inner_right, c > 0))(functools.partial(send_item, i, h, False))
         pl.when(jnp.logical_and(jnp.logical_not(inner_right), c + 1 < n))(
-            lambda: ag_copy(first_mine + i, h, True).start())
+            functools.partial(send_item, i, h, True))
 
     cols = acc.shape[1]
     tile = sz["tile"]
@@ -361,10 +380,11 @@
         @pl.when(jnp.logical_and(jnp.logical_and(b >= 0, b < n), jnp.logical_and(i >= 0, i < count(b))))
         def _():
             q = begin(b) + i
-            with jax.named_scope("take"):
-                ag_copy(q, h, right).wait_recv()
             more = c + 1 < n if right else c > 0
-            pl.when(more)(lambda: ag_copy(q, h, right).start())
+            for p in parts_of(h):
+                with jax.named_scope("take"):
+                    ag_copy(q, p, right).wait_recv()
+                pl.when(more)(lambda: ag_copy(q, p, right).start())
             project(q, rows_half(h))
 
     def arrive_all(d, low, high, h):
@@ -414,7 +434,9 @@
         for i in range(sz["release"]):
             arrive_inward(i, away)
             arrive_inward(i, stay)
-        send_far()
+            for k in range(ends):
+                if i == sz["release"] - 1 - (ends - 1 - k) * sz["gap"]:
+                    send_far(k)
         pl.when(c == 0)(functools.partial(forward_others, 3, 1))
         pl.when(c == n - 1)(functools.partial(forward_others, 1, 3))
         forward_weights(0)
@@ -496,7 +518,8 @@
             pl.when(at_end)(functools.partial(sent, i, n - 2))
             pl.when(jnp.logical_not(at_end))(functools.partial(sent, i, n - 3))
     for kind in (0, 5):
-        take(key_bytes(kind, (n - 1) * share), s_k.at[kind // 5])
+        pl.when(at_end)(lambda: take(key_bytes(kind, 2 * share), s_k.at[kind // 5]))
+        pl.when(jnp.logical_not(at_end))(lambda: take(key_bytes(kind, 4 * share), s_k.at[kind // 5]))
         take(key_bytes(kind, (n - 1) * (tps - 1) * share), s_t.at[kind // 5])
     take(pos.at[pl.ds(0, n - 1)], s_k.at[2])
     arrive_all(2, 0, mids, stay)
@@ -569,7 +592,7 @@
             dma((2,)),
             dma((2,)),
             dma((2,)),
-            dma((chunks, 2)),
+            dma((chunks, 3)),
             dma,
             dma((3, 2)),
             pltpu.SemaphoreType.REGULAR((2,)),
@@ -635,7 +658,9 @@
 
 CHUNK_HEADS = 2
 END_CHUNKS = 2
-RELEASE = 3
+RELEASE = 4
+SPREAD = 2
+GAP = 2
 EARLY = 1
 BEHIND = 1
 
@@ -648,7 +673,7 @@
     ends = END_CHUNKS * chunks // 16
     mids = chunks // 2 - ends
     sz = dict(n=n, g=groups, t=tps, hc=CHUNK_HEADS, ends=ends, mids=mids, tok=q_nope.shape[0],
-              release=RELEASE, early=EARLY, behind=BEHIND,
+              release=RELEASE, spread=SPREAD, gap=GAP, early=EARLY, behind=BEHIND,
               nope=w_uk.shape[1] * n, rope=k_rope.shape[1], lat=c_kv.shape[1],
               vdim=w_uv.shape[2], tile=w_out.shape[1] // 2)
     seq = n * sz["tok"]
@@ -660,7 +685,8 @@
         and CHUNK_HEADS % groups == 0
         and groups == 2
         and mids >= ends > EARLY
-        and mids > RELEASE
+        and mids > RELEASE > (ends - 1) * GAP
+        and mids - 1 > (ends - 1) * SPREAD
         and mids >= n + 1
         and sz["nope"] == sz["vdim"]
         and seq <= 512

time: 79 us -> 77.6 us (0.982)
  Pallas kernels: 78.1 us -> 76.7 us
    pallas_call x1, Pallas kernels: 78.1 us -> 76.7 us  [fast(): pl.pallas_call(functools.partial(mega, sz), out_shape=pltpu.VMEM((seq //...]
where the time goes in v5:
time: 77.6 us; the launch traced here: 77.4 us
  Pallas kernels  76.7 us (99%)
    pallas_call x1, Pallas kernels, fast(): pl.pallas_call(functools.partial(mega, sz), out_shape=pltpu.VMEM((seq //...  76.7 us

profile of v5, /device:TPU:0, one launch (start us, length us, event | category | flops | bytes accessed | tf_op | source)
XLA Modules:
  0.0 77.4 jit_solution(3135973452178924632)
XLA Ops:
  0.0 76.7 %shard_map.82 = bf16[64,1792]{1,0:T(8,128)(2,1)S(1)} custom-call(bf16[64,4096]{1,0:T(8,128)(2,1)} %qn_in.1, bf16[64,2048]{1,0:T(8,128)(2,1)} %qr_in.1, bf16[64,512]{1,0:T(8,128)(2,1)} %kv_in.1, bf16[64,64]{1,0:T(8,128)(2,1)} %kr_in.1, s32[1,64]{1,0:T(1,128)} %bitcast.1, bf16[32,32,512]{2,1,0:T(8,128)(2,1)} %wuk_in.1, bf16[32,128,128]{2,1,0:T(8,128)(2,1)} %wuv_in.1, ...), custom_call_target="tpu_custom_call" | custom-call | tf_op jit(solution)/shard_map/pallas_call | solution.py:562
  76.7 0.7 copy.10

commit v6 on v5

--- a/solution.py
+++ b/solution.py
@@ -540,13 +540,13 @@
     for k, at in enumerate(spans):
         part[0, :, at] = block(mate, at).astype(BF16)
         rs_copy(2, k).start()
+    drain()
     for k, at in enumerate(spans):
         rs_copy(1, k).wait_recv()
         own = block(t, at) + got[2, :, at].astype(F32)
         rs_copy(2, k).wait_recv()
         out_ref[:, at] = (own + got[0, :, at].astype(F32)).astype(BF16)
     take(part, s_rs)
-    drain()
 
 
 def fast(sz, q_nope, q_rope, c_kv, k_rope, positions, w_uk, w_uv, w_out):

time: 77.6 us -> 77.6 us (level)
  no operation moved by 1% of the time
where the time goes in v6:
time: 77.6 us; the launch traced here: 77.4 us
  Pallas kernels  76.7 us (99%)
    pallas_call x1, Pallas kernels, fast(): pl.pallas_call(functools.partial(mega, sz), out_shape=pltpu.VMEM((seq //...  76.7 us

profile of v6, /device:TPU:0, one launch (start us, length us, event | category | flops | bytes accessed | tf_op | source)
XLA Modules:
  0.0 77.4 jit_solution(7993907747264144276)
XLA Ops:
  0.0 76.7 %shard_map.82 = bf16[64,1792]{1,0:T(8,128)(2,1)S(1)} custom-call(bf16[64,4096]{1,0:T(8,128)(2,1)} %qn_in.1, bf16[64,2048]{1,0:T(8,128)(2,1)} %qr_in.1, bf16[64,512]{1,0:T(8,128)(2,1)} %kv_in.1, bf16[64,64]{1,0:T(8,128)(2,1)} %kr_in.1, s32[1,64]{1,0:T(1,128)} %bitcast.1, bf16[32,32,512]{2,1,0:T(8,128)(2,1)} %wuk_in.1, bf16[32,128,128]{2,1,0:T(8,128)(2,1)} %wuv_in.1, ...), custom_call_target="tpu_custom_call" | custom-call | tf_op jit(solution)/shard_map/pallas_call | solution.py:562
  76.7 0.7 copy.10
